TPU v7x, 128 devices: a whole 4x4x4 slice. The times are simulated.
128 devices in a mesh: section: 2 (over x_hi), dp: 16 (over z, y), mp: 4 (over x_lo, core).
Axes of the slice: x: 4 (x_hi: 2, x_lo: 2; x = x_hi * 2 + x_lo), y: 4, z: 4, core: 2. Of those that a mesh axis runs over, the one named last changes fastest.
Arguments:
- text_feats: bfloat16 [16384, 512], P('dp'), may hold values from -48 to 48
- image_feats: bfloat16 [16384, 512], P(('dp', 'mp')), may hold values from -48 to 48
- logit_scale: float32 [1], replicated, may hold values from 10 to 320
- layer_inputs: bfloat16 [2, 16384, 512], P('section', 'dp'), may hold values from -6 to 6
- w_in: bfloat16 [2, 512, 2048], P('section', None, 'mp'), may hold values from -0.25 to 0.25
- w_out: bfloat16 [2, 2048, 512], P('section', 'mp'), may hold values from -0.125 to 0.125
Outputs:
- image_grad: bfloat16 [16384, 512], P(('dp', 'mp'))
- input_grad: bfloat16 [16384, 512], P('dp', 'section')
- w_in_grad: float32 [2, 512, 2048], P('section', 'dp', 'mp')
- w_out_grad_t: float32 [2, 512, 2048], P('section', 'dp', 'mp')
All inputs are finite; a program needn't handle non-finite values.
Results may differ from a plain program's by a relative error of at most 0.017.
Values may be sent and summed in bfloat16 or wider, within the bound.
A program may use at most 128 MiB of HBM per device.

v0:
```python
import jax
import jax.numpy as jnp
from jax import lax
from jax.sharding import PartitionSpec as P

MICRO = 4


def from_everyone(array, axis):
    copies = jnp.broadcast_to(array, (lax.axis_size(axis), *array.shape))
    return lax.all_to_all(copies, axis, split_axis=0, concat_axis=0, tiled=True)


def collected_together(array, axis):
    leaves = jax.tree.leaves(array)
    sequence = sorted(range(len(leaves)), key=lambda k: -leaves[k].size)
    width = (1, *leaves[sequence[0]].shape)[-1]
    lines = [
        jnp.pad(leaves[k].reshape(-1), (0, -leaves[k].size % width)).reshape(-1, width)
        for k in sequence
    ]
    both, at, found = (from_everyone(jnp.concatenate(lines), axis), 0, {})
    for k, line in zip(sequence, lines):
        slab = both[:, at : at + len(line)].reshape(len(both), -1)
        found[k] = slab[:, : leaves[k].size].reshape(-1, *leaves[k].shape)
        at += len(line)
    numbers = iter(range(len(leaves)))
    return jax.tree.map(lambda _: found[next(numbers)], array)


def combined_pairwise(pieces, combine):
    while len(jax.tree.leaves(pieces)[0]) > 1:
        pieces = jax.vmap(combine)(
            *(jax.tree.map(lambda part: part[side::2], pieces) for side in (0, 1))
        )
    return jax.tree.map(lambda part: part[0], pieces)


def joined_all(array, axis, combine):
    pieces = collected_together(array, axis)
    return combined_pairwise(pieces, combine)


def of_everyone(array, axis):
    return from_everyone(array, axis).astype(jnp.float32).sum(axis=0)


def shifted(block, axis, distance):
    devices = range(lax.axis_size(axis))
    route = [(i - distance, i) for i in devices if i - distance in devices]
    return lax.ppermute(block, axis, route)


def picked(array, axis, root):
    return lax.dynamic_index_in_dim(lax.all_gather(array, axis), root, 0, keepdims=False)


def in_one_piece(arrays, axis, dim, along):
    both = jnp.concatenate(arrays, axis=along)
    result, at, done = (lax.psum_scatter(both, axis, scatter_dimension=dim, tiled=True), 0, [])
    for a in arrays:
        done.append(lax.slice_in_dim(result, at, at + a.shape[along], axis=along))
        at += a.shape[along]
    return tuple(done)


def unit_rows(values):
    wide = values.astype(jnp.float32)
    length = jnp.sqrt(jnp.sum(wide * wide, axis=1, keepdims=True) + 1.0)
    return (wide / length, length)


def unit_backward(unit, length, grad_unit):
    return (grad_unit - unit * jnp.sum(unit * grad_unit, axis=1, keepdims=True)) / length


def quick_gelu(values):
    return values * jax.nn.sigmoid(1.702 * values)


def quick_slope(values):
    sigm = jax.nn.sigmoid(1.702 * values)
    return sigm + 1.702 * values * sigm * (1.0 - sigm)


def joined_softmax(left_pair, right_pair):
    peak_value = jnp.maximum(left_pair[0], right_pair[0])
    total = left_pair[1] * jnp.exp(left_pair[0] - peak_value) + right_pair[1] * jnp.exp(
        right_pair[0] - peak_value
    )
    return (peak_value, total)


def contract_rows(left_side, right_side):
    return lax.dot_general(
        left_side, right_side, (((0,), (0,)), ((), ())), preferred_element_type=jnp.float32
    )


def contract_cols(left_side, right_side):
    return lax.dot_general(
        left_side, right_side, (((1,), (1,)), ((), ())), preferred_element_type=jnp.float32
    )


def body(text_feats, image_feats, logit_scale, layer_inputs, w_in, w_out):
    logit_mult = logit_scale[0]
    mp_count = lax.axis_size("mp")
    segment_count = lax.axis_size("section")
    dp_index = lax.axis_index("dp")
    mp_index = lax.axis_index("mp")
    segment_index = lax.axis_index("section")
    row_count = text_feats.shape[0]
    own_rows = image_feats.shape[0]
    text_unit, text_length = unit_rows(text_feats)
    image_unit, image_length = unit_rows(image_feats)
    text_low = text_unit.astype(jnp.bfloat16)
    image_low = image_unit.astype(jnp.bfloat16)
    columns = lax.all_gather(image_low, "dp", axis=0, tiled=True)
    column_total_count = columns.shape[0]
    scores = logit_mult * contract_cols(text_low, columns)
    text_ids = dp_index * row_count + jnp.arange(row_count, dtype=jnp.int32)
    column_pos = jnp.arange(column_total_count, dtype=jnp.int32)
    image_ids = (column_pos // own_rows * mp_count + mp_index) * own_rows + column_pos % own_rows
    positive = (text_ids[:, None] == image_ids[None, :]).astype(jnp.float32)
    local_rpeak = jnp.max(scores, axis=1)
    local_cpeak = jnp.max(scores, axis=0)
    row_peak, row_total = joined_all(
        (local_rpeak, jnp.sum(jnp.exp(scores - local_rpeak[:, None]), axis=1)), "mp", joined_softmax
    )
    column_local = jnp.sum(jnp.exp(scores - local_cpeak[None, :]), axis=0)
    column_peak, column_total = joined_all((local_cpeak, column_local), "dp", joined_softmax)
    row_prob = jnp.exp(scores - row_peak[:, None]) / row_total[:, None]
    column_prob = jnp.exp(scores - column_peak[None, :]) / column_total[None, :]
    score_grad = (0.5 * (row_prob + column_prob) - positive).astype(jnp.bfloat16)
    text_share = logit_mult * jnp.dot(score_grad, columns, preferred_element_type=jnp.float32)
    text_unit_grad = of_everyone(text_share.astype(jnp.bfloat16), "mp").astype(jnp.float32)
    top_grad = unit_backward(text_unit, text_length, text_unit_grad).astype(jnp.bfloat16)
    image_unit_grad = lax.psum_scatter(
        (logit_mult * contract_rows(score_grad, text_low)).astype(jnp.bfloat16),
        "dp",
        scatter_dimension=0,
        tiled=True,
    ).astype(jnp.float32)
    image_grad = unit_backward(image_unit, image_length, image_unit_grad).astype(jnp.bfloat16)
    segment_inputs = layer_inputs[0]
    w_first = w_in[0]
    w_second = w_out[0]
    step_rows = row_count // MICRO
    last_segment = segment_count - 1
    time_steps = MICRO + segment_count - 1
    is_last = segment_index == last_segment
    is_first = segment_index == 0
    incoming = jnp.zeros((step_rows, segment_inputs.shape[1]), jnp.bfloat16)
    grad_first = jnp.zeros(w_first.shape, jnp.float32)
    grad_second = jnp.zeros(w_first.shape, jnp.float32)
    finished = jnp.zeros((row_count, segment_inputs.shape[1]), jnp.bfloat16)
    for time_step in range(time_steps):
        micro_slot = time_step - last_segment + segment_index
        active = jnp.logical_and(micro_slot >= 0, micro_slot < MICRO)
        row_start = jnp.clip(micro_slot, 0, MICRO - 1) * step_rows
        top_start = min(time_step, MICRO - 1) * step_rows
        top_piece = top_grad[top_start : top_start + step_rows]
        grad_now = jnp.where(is_last, top_piece, incoming)
        inputs_now = lax.dynamic_slice_in_dim(segment_inputs, row_start, step_rows, 0)
        pre_act = jnp.dot(inputs_now, w_first, preferred_element_type=jnp.float32)
        activation = quick_gelu(pre_act).astype(jnp.bfloat16)
        back_grad = contract_cols(grad_now, w_second)
        pre_grad = (back_grad * quick_slope(pre_act)).astype(jnp.bfloat16)
        unit_share = contract_cols(pre_grad, w_first)
        summed = of_everyone(unit_share.astype(jnp.bfloat16), "mp").astype(jnp.float32)
        grad_prev = (grad_now.astype(jnp.float32) + summed).astype(jnp.bfloat16)
        weight = active.astype(jnp.float32)
        grad_first = grad_first + weight * contract_rows(inputs_now, pre_grad)
        grad_second = grad_second + weight * contract_rows(grad_now, activation)
        updated = lax.dynamic_update_slice_in_dim(finished, grad_prev, row_start, 0)
        finished = jnp.where(jnp.logical_and(active, is_first), updated, finished)
        if time_step + 1 < time_steps:
            incoming = shifted(grad_prev, "section", -1)
    whole_grad = picked(finished, "section", 0)
    feature_width = whole_grad.shape[1] // segment_count
    feature_start = segment_index * feature_width
    input_grad = lax.dynamic_slice_in_dim(whole_grad, feature_start, feature_width, 1)
    first_sum, second_sum = tuple(
        (
            part.astype(jnp.float32)
            for part in in_one_piece(
                (grad_first.astype(jnp.bfloat16), grad_second.astype(jnp.bfloat16)), "dp", 0, 1
            )
        )
    )
    return (image_grad, input_grad, first_sum[None], second_sum[None])


def solution(mesh):
    placed = (
        P("dp", None),
        P(("dp", "mp"), None),
        P(),
        P("section", "dp", None),
        P("section", None, "mp"),
        P("section", "mp", None),
    )
    return jax.shard_map(
        body,
        mesh=mesh,
        in_specs=placed,
        out_specs=(
            P(("dp", "mp"), None),
            P("dp", "section"),
            P("section", "dp", "mp"),
            P("section", "dp", "mp"),
        ),
        check_vma=False,
    )
```

profile of v0, /device:TPU:1, one launch (start us, length us, event | category | flops | bytes accessed | tf_op | source)
XLA Modules:
  0.0 463.0 jit_solution(3558980149796986611)
XLA Ops:
  12.4 52.9 %all-gather.3.cloned.1.call-done = bf16[4096,512]{1,0:T(8,128)(2,1)} async-done(((bf16[256,512]{1,0:T(8,128)(2,1)}), bf16[4096,512]{1,0:T(8,128)(2,1)}) %all-gather.3.cloned.1.call-update) | async-done | bytes 4194320 | tf_op jit(solution)/shard_map/all_gather | solution.py:119
  65.3 6.8 %multiply_reduce_fusion.1 = (f32[1024]{0:T(1024)S(1)}, f32[1024,4096]{1,0:T(8,128)S(1)}) fusion(f32[]{:T(128)} %bitcast.111, bf16[4096,512]{1,0:T(8,128)(2,1)} %all-gather.3.cloned.1.call-done, f32[1024]{0:T(1024)S(1)} %add_sqrt_fusion, bf16[1024,512]{1,0:T(8,128)(2,1)} %param.6), kind=kOutput, calls=%fused_computation.4 | convolution fusion | flops 4304927744 | bytes 22028292 | tf_op jit(solution)/shard_map/dot_general | solution.py:101
  82.6 8.5 %exponential_reduce_fusion = f32[4096]{0:T(1024)S(1)} fusion(f32[1024,4096]{1,0:T(8,128)} %copy-done.1, f32[4096]{0:T(1024)S(1)} %get-tuple-element.17, f32[]{:T(128)} %bitcast.115), kind=kLoop, calls=%fused_computation.1 | loop fusion | flops 12578816 | bytes 16809988 | tf_op jit(solution)/shard_map/reduce_sum | solution.py:131
  92.1 5.0 %all-to-all-start.1 = ((f32[16,2,4096]{2,1,0:T(2,128)}), f32[16,2,4096]{2,1,0:T(2,128)S(1)}, u32[]{:S(2)}, u32[]{:S(2)}) async-start(f32[16,2,4096]{2,1,0:T(2,128)} %broadcast_in_dim.51), calls=%async_computation.1 | async-start | bytes 1048576 | tf_op jit(solution)/shard_map/all_to_all | solution.py:11
  97.4 10.8 %all-to-all-done.1 = f32[16,2,4096]{2,1,0:T(2,128)S(1)} async-done(((f32[16,2,4096]{2,1,0:T(2,128)}), f32[16,2,4096]{2,1,0:T(2,128)S(1)}, u32[]{:S(2)}, u32[]{:S(2)}) %all-to-all-start.1) | async-done | bytes 524320 | tf_op jit(solution)/shard_map/all_to_all | solution.py:11
  110.7 11.4 %subtract_convert_fusion = bf16[1024,4096]{1,0:T(8,128)(2,1)S(1)} fusion(f32[1024,4096]{1,0:T(8,128)} %copy-done.1, s32[4096]{0:T(1024)S(1)} %fusion.87, f32[4096]{0:T(1024)S(1)} %bitcast.117, f32[4096]{0:T(1024)S(1)} %bitcast.118, f32[1024]{0:T(1024)S(1)} %bitcast.120, f32[1024]{0:T(1024)S(1)} %bitcast.121, f32[]{:T(128)} %bitcast.114, s32[1024]{0:T(1024)S(1)} %iota_add_fusion), kind=kLoop, calls=%fused_computation | loop fusion | flops 46137344 | bytes 25227268 | tf_op jit(solution)/shard_map/convert_element_type | solution.py:135
  132.1 6.5 %all-to-all-start.2 = ((bf16[4,1024,512]{2,1,0:T(8,128)(2,1)}), bf16[4,1024,512]{2,1,0:T(8,128)(2,1)}, u32[]{:S(2)}, u32[]{:S(2)}) async-start(bf16[4,1024,512]{2,1,0:T(8,128)(2,1)} %broadcast_in_dim.53), calls=%async_computation.3 | async-start | bytes 8388608 | tf_op jit(solution)/shard_map/all_to_all | solution.py:11
  139.0 47.0 %all-to-all-done.2 = bf16[4,1024,512]{2,1,0:T(8,128)(2,1)} async-done(((bf16[4,1024,512]{2,1,0:T(8,128)(2,1)}), bf16[4,1024,512]{2,1,0:T(8,128)(2,1)}, u32[]{:S(2)}, u32[]{:S(2)}) %all-to-all-start.2) | async-done | bytes 4194336 | tf_op jit(solution)/shard_map/all_to_all | solution.py:11
  193.7 5.2 %all-to-all-start.3 = ((bf16[4,256,512]{2,1,0:T(8,128)(2,1)}), bf16[4,256,512]{2,1,0:T(8,128)(2,1)}, u32[]{:S(2)}, u32[]{:S(2)}) async-start(bf16[4,256,512]{2,1,0:T(8,128)(2,1)} %broadcast_in_dim.55), calls=%async_computation.4 | async-start | bytes 2097152 | tf_op jit(solution)/shard_map/all_to_all | solution.py:11
  199.2 13.3 %all-to-all-done.3 = bf16[4,256,512]{2,1,0:T(8,128)(2,1)} async-done(((bf16[4,256,512]{2,1,0:T(8,128)(2,1)}), bf16[4,256,512]{2,1,0:T(8,128)(2,1)}, u32[]{:S(2)}, u32[]{:S(2)}) %all-to-all-start.3) | async-done | bytes 1048608 | tf_op jit(solution)/shard_map/all_to_all | solution.py:11
  218.2 9.9 %multiply_convert_fusion = bf16[4096,512]{1,0:T(8,128)(2,1)} fusion(bf16[1024,4096]{1,0:T(8,128)(2,1)} %copy-done.4, f32[]{:T(128)} %bitcast.110, bf16[1024,512]{1,0:T(8,128)(2,1)S(1)} %copy-done.3, f32[1024]{0:T(1024)S(1)} %add_sqrt_fusion), kind=kOutput, calls=%fused_computation.6 | convolution fusion | flops 4300734464 | bytes 13635588 | tf_op jit(solution)/shard_map/dot_general | solution.py:95
  232.9 5.2 %all-to-all-start.4 = ((bf16[4,256,512]{2,1,0:T(8,128)(2,1)}), bf16[4,256,512]{2,1,0:T(8,128)(2,1)}, u32[]{:S(2)}, u32[]{:S(2)}) async-start(bf16[4,256,512]{2,1,0:T(8,128)(2,1)} %broadcast_in_dim.56), calls=%async_computation.5 | async-start | bytes 2097152 | tf_op jit(solution)/shard_map/all_to_all | solution.py:11
  238.1 13.6 %all-to-all-done.4 = bf16[4,256,512]{2,1,0:T(8,128)(2,1)} async-done(((bf16[4,256,512]{2,1,0:T(8,128)(2,1)}), bf16[4,256,512]{2,1,0:T(8,128)(2,1)}, u32[]{:S(2)}, u32[]{:S(2)}) %all-to-all-start.4) | async-done | bytes 1048608 | tf_op jit(solution)/shard_map/all_to_all | solution.py:11
  256.6 9.9 %collective-permute-done.1 = bf16[256,512]{1,0:T(8,128)(2,1)} collective-permute-done((bf16[256,512]{1,0:T(8,128)(2,1)}, bf16[256,512]{1,0:T(8,128)(2,1)}, u32[]{:S(2)}, u32[]{:S(2)}) %collective-permute-start.1) | collective-permute-done | bytes 262176 | tf_op jit(solution)/shard_map/ppermute | solution.py:51
  271.1 5.7 %all-to-all-start.5 = ((bf16[4,256,512]{2,1,0:T(8,128)(2,1)}), bf16[4,256,512]{2,1,0:T(8,128)(2,1)}, u32[]{:S(2)}, u32[]{:S(2)}) async-start(bf16[4,256,512]{2,1,0:T(8,128)(2,1)} %broadcast_in_dim.57), calls=%async_computation.6 | async-start | bytes 2097152 | tf_op jit(solution)/shard_map/all_to_all | solution.py:11
  283.7 6.6 %all-to-all-done.5 = bf16[4,256,512]{2,1,0:T(8,128)(2,1)} async-done(((bf16[4,256,512]{2,1,0:T(8,128)(2,1)}), bf16[4,256,512]{2,1,0:T(8,128)(2,1)}, u32[]{:S(2)}, u32[]{:S(2)}) %all-to-all-start.5) | async-done | bytes 1048608 | tf_op jit(solution)/shard_map/all_to_all | solution.py:11
  297.7 6.2 %collective-permute-done.2 = bf16[256,512]{1,0:T(8,128)(2,1)S(1)} collective-permute-done((bf16[256,512]{1,0:T(8,128)(2,1)S(1)}, bf16[256,512]{1,0:T(8,128)(2,1)S(1)}, u32[]{:S(2)}, u32[]{:S(2)}) %collective-permute-start.2) | collective-permute-done | bytes 262176 | tf_op jit(solution)/shard_map/ppermute | solution.py:51
  308.4 6.0 %all-to-all-start.6 = ((bf16[4,256,512]{2,1,0:T(8,128)(2,1)}), bf16[4,256,512]{2,1,0:T(8,128)(2,1)}, u32[]{:S(2)}, u32[]{:S(2)}) async-start(bf16[4,256,512]{2,1,0:T(8,128)(2,1)} %broadcast_in_dim.58), calls=%async_computation.7 | async-start | bytes 2097152 | tf_op jit(solution)/shard_map/all_to_all | solution.py:11
  319.6 8.3 %all-to-all-done.6 = bf16[4,256,512]{2,1,0:T(8,128)(2,1)} async-done(((bf16[4,256,512]{2,1,0:T(8,128)(2,1)}), bf16[4,256,512]{2,1,0:T(8,128)(2,1)}, u32[]{:S(2)}, u32[]{:S(2)}) %all-to-all-start.6) | async-done | bytes 1048608 | tf_op jit(solution)/shard_map/all_to_all | solution.py:11
  334.1 7.5 %collective-permute-done.3 = bf16[256,512]{1,0:T(8,128)(2,1)S(1)} collective-permute-done((bf16[256,512]{1,0:T(8,128)(2,1)S(1)}, bf16[256,512]{1,0:T(8,128)(2,1)S(1)}, u32[]{:S(2)}, u32[]{:S(2)}) %collective-permute-start.3) | collective-permute-done | bytes 262176 | tf_op jit(solution)/shard_map/ppermute | solution.py:51
  348.5 5.3 %all-to-all-start.7 = ((bf16[4,256,512]{2,1,0:T(8,128)(2,1)}), bf16[4,256,512]{2,1,0:T(8,128)(2,1)S(1)}, u32[]{:S(2)}, u32[]{:S(2)}) async-start(bf16[4,256,512]{2,1,0:T(8,128)(2,1)} %broadcast_in_dim.59), calls=%async_computation.8 | async-start | bytes 2097152 | tf_op jit(solution)/shard_map/all_to_all | solution.py:11
  356.0 11.3 %all-to-all-done.7 = bf16[4,256,512]{2,1,0:T(8,128)(2,1)S(1)} async-done(((bf16[4,256,512]{2,1,0:T(8,128)(2,1)}), bf16[4,256,512]{2,1,0:T(8,128)(2,1)S(1)}, u32[]{:S(2)}, u32[]{:S(2)}) %all-to-all-start.7) | async-done | bytes 1048608 | tf_op jit(solution)/shard_map/all_to_all | solution.py:11
  372.4 42.6 %reduce-scatter.7.cloned.1.call-done = bf16[32,1024]{1,0:T(8,128)(2,1)} async-done(((bf16[512,1024]{1,0:T(8,128)(2,1)}), bf16[32,1024]{1,0:T(8,128)(2,1)}) %reduce-scatter.7.cloned.1.call-update) | async-done | bytes 65552
  417.5 36.8 %all-gather.5.cloned.1.call-done = bf16[2,1024,512]{2,1,0:T(8,128)(2,1)} async-done(((bf16[1,1024,512]{2,1,0:T(8,128)(2,1)}), bf16[2,1024,512]{2,1,0:T(8,128)(2,1)}) %all-gather.5.cloned.1.call-update) | async-done | bytes 2097168 | tf_op jit(solution)/shard_map/all_gather | solution.py:55
  (166 shorter events, 105.5 us)
Async XLA Ops:
  7.2 131.5 %copy-start = (bf16[1,1024,512]{2,1,0:T(8,128)(2,1)S(1)}, bf16[1,1024,512]{2,1,0:T(8,128)(2,1)}, u32[]{:S(2)}) copy-start(bf16[1,1024,512]{2,1,0:T(8,128)(2,1)} %param.9) | copy-start | bytes 3145732
  7.2 58.1 %all-gather.3.cloned.1.call-start = ((), (), s32[]{:S(2)}) async-start(), calls=%async_computation.10 | async-start | bytes 4456448 | tf_op jit(solution)/shard_map/all_gather | solution.py:119
  78.5 12.6 %all-to-all-start = ((f32[4,2,1024]{2,1,0:T(2,128)}), f32[4,2,1024]{2,1,0:T(2,128)S(1)}, u32[]{:S(2)}, u32[]{:S(2)}) async-start(f32[4,2,1024]{2,1,0:T(2,128)} %broadcast_in_dim.50), calls=%async_computation | async-start | bytes 65536 | tf_op jit(solution)/shard_map/all_to_all | solution.py:11
  92.1 16.0 %all-to-all-start.1 = ((f32[16,2,4096]{2,1,0:T(2,128)}), f32[16,2,4096]{2,1,0:T(2,128)S(1)}, u32[]{:S(2)}, u32[]{:S(2)}) async-start(f32[16,2,4096]{2,1,0:T(2,128)} %broadcast_in_dim.51), calls=%async_computation.1 | async-start | bytes 1048576 | tf_op jit(solution)/shard_map/all_to_all | solution.py:11
  132.1 57.0 %copy-start.3 = (bf16[1024,512]{1,0:T(8,128)(2,1)S(1)}, bf16[1024,512]{1,0:T(8,128)(2,1)}, u32[]{:S(2)}) copy-start(bf16[1024,512]{1,0:T(8,128)(2,1)} %param.6) | copy-start | bytes 3145732
  132.1 53.8 %all-to-all-start.2 = ((bf16[4,1024,512]{2,1,0:T(8,128)(2,1)}), bf16[4,1024,512]{2,1,0:T(8,128)(2,1)}, u32[]{:S(2)}, u32[]{:S(2)}) async-start(bf16[4,1024,512]{2,1,0:T(8,128)(2,1)} %broadcast_in_dim.53), calls=%async_computation.3 | async-start | bytes 8388608 | tf_op jit(solution)/shard_map/all_to_all | solution.py:11
  139.0 52.6 %copy-start.19 = (f32[256,512]{1,0:T(8,128)}, f32[256,512]{1,0:T(8,128)S(1)}, u32[]{:S(2)}) copy-start(f32[256,512]{1,0:T(8,128)S(1)} %fusion.33) | copy-start | bytes 1572868
  193.7 18.8 %all-to-all-start.3 = ((bf16[4,256,512]{2,1,0:T(8,128)(2,1)}), bf16[4,256,512]{2,1,0:T(8,128)(2,1)}, u32[]{:S(2)}, u32[]{:S(2)}) async-start(bf16[4,256,512]{2,1,0:T(8,128)(2,1)} %broadcast_in_dim.55), calls=%async_computation.4 | async-start | bytes 2097152 | tf_op jit(solution)/shard_map/all_to_all | solution.py:11
  198.9 170.4 %reduce-scatter.5.cloned.1.call-start = ((), (), s32[]{:S(2)}) async-start(), calls=%async_computation.11 | async-start | bytes 4456448 | tf_op jit(solution)/shard_map/reduce_scatter | solution.py:139
  199.2 30.1 %copy-start.20 = (f32[256,512]{1,0:T(8,128)}, f32[256,512]{1,0:T(8,128)S(1)}, u32[]{:S(2)}) copy-start(f32[256,512]{1,0:T(8,128)S(1)} %fusion.30) | copy-start | bytes 1572868
  216.7 11.4 %collective-permute-start = (bf16[256,512]{1,0:T(8,128)(2,1)S(1)}, bf16[256,512]{1,0:T(8,128)(2,1)}, u32[]{:S(2)}, u32[]{:S(2)}) collective-permute-start(bf16[256,512]{1,0:T(8,128)(2,1)S(1)} %get-tuple-element.25), channel_id=1, source_target_pairs={{64,0},{65,1},{66,2},{67,3},{68,4},{69,5},{70,6},{71,7},{72,8},{73... | collective-permute-start | bytes 786440 | tf_op jit(solution)/shard_map/ppermute | solution.py:51
  228.1 38.4 %copy-start.6 = (bf16[1024,512]{1,0:T(8,128)(2,1)S(1)}, bf16[1024,512]{1,0:T(8,128)(2,1)}, u32[]{:S(2)}) copy-start(bf16[1024,512]{1,0:T(8,128)(2,1)} %copy-done.5) | copy-start | bytes 3145732
  229.3 27.3 %copy-start.14 = (bf16[256,512]{1,0:T(8,128)(2,1)}, bf16[256,512]{1,0:T(8,128)(2,1)S(1)}, u32[]{:S(2)}) copy-start(bf16[256,512]{1,0:T(8,128)(2,1)S(1)} %slice_select_fusion.1) | copy-start | bytes 786436
  232.9 18.7 %all-to-all-start.4 = ((bf16[4,256,512]{2,1,0:T(8,128)(2,1)}), bf16[4,256,512]{2,1,0:T(8,128)(2,1)}, u32[]{:S(2)}, u32[]{:S(2)}) async-start(bf16[4,256,512]{2,1,0:T(8,128)(2,1)} %broadcast_in_dim.56), calls=%async_computation.5 | async-start | bytes 2097152 | tf_op jit(solution)/shard_map/all_to_all | solution.py:11
  255.0 11.5 %collective-permute-start.1 = (bf16[256,512]{1,0:T(8,128)(2,1)}, bf16[256,512]{1,0:T(8,128)(2,1)}, u32[]{:S(2)}, u32[]{:S(2)}) collective-permute-start(bf16[256,512]{1,0:T(8,128)(2,1)} %get-tuple-element.23), channel_id=1, source_target_pairs={{64,0},{65,1},{66,2},{67,3},{68,4},{69,5},{70,6},{71,7},{72,8},{73... | collective-permute-start | bytes 786440 | tf_op jit(solution)/shard_map/ppermute | solution.py:51
  271.1 19.3 %all-to-all-start.5 = ((bf16[4,256,512]{2,1,0:T(8,128)(2,1)}), bf16[4,256,512]{2,1,0:T(8,128)(2,1)}, u32[]{:S(2)}, u32[]{:S(2)}) async-start(bf16[4,256,512]{2,1,0:T(8,128)(2,1)} %broadcast_in_dim.57), calls=%async_computation.6 | async-start | bytes 2097152 | tf_op jit(solution)/shard_map/all_to_all | solution.py:11
  293.6 10.3 %collective-permute-start.2 = (bf16[256,512]{1,0:T(8,128)(2,1)S(1)}, bf16[256,512]{1,0:T(8,128)(2,1)S(1)}, u32[]{:S(2)}, u32[]{:S(2)}) collective-permute-start(bf16[256,512]{1,0:T(8,128)(2,1)S(1)} %get-tuple-element.21), channel_id=1, source_target_pairs={{64,0},{65,1},{66,2},{67,3},{68,4},{69,5},{70,6},{71,7},{72,8},{73... | collective-permute-start | bytes 786440 | tf_op jit(solution)/shard_map/ppermute | solution.py:51
  308.4 19.6 %all-to-all-start.6 = ((bf16[4,256,512]{2,1,0:T(8,128)(2,1)}), bf16[4,256,512]{2,1,0:T(8,128)(2,1)}, u32[]{:S(2)}, u32[]{:S(2)}) async-start(bf16[4,256,512]{2,1,0:T(8,128)(2,1)} %broadcast_in_dim.58), calls=%async_computation.7 | async-start | bytes 2097152 | tf_op jit(solution)/shard_map/all_to_all | solution.py:11
  314.3 100.6 %reduce-scatter.7.cloned.1.call-start = ((), (), s32[]{:S(2)}) async-start(), calls=%async_computation.13 | async-start | bytes 1114112
  331.3 10.3 %collective-permute-start.3 = (bf16[256,512]{1,0:T(8,128)(2,1)S(1)}, bf16[256,512]{1,0:T(8,128)(2,1)S(1)}, u32[]{:S(2)}, u32[]{:S(2)}) collective-permute-start(bf16[256,512]{1,0:T(8,128)(2,1)S(1)} %get-tuple-element.19), channel_id=1, source_target_pairs={{64,0},{65,1},{66,2},{67,3},{68,4},{69,5},{70,6},{71,7},{72,8},{73... | collective-permute-start | bytes 786440 | tf_op jit(solution)/shard_map/ppermute | solution.py:51
  344.6 22.9 %copy-start.16 = (bf16[256,512]{1,0:T(8,128)(2,1)S(1)}, bf16[256,512]{1,0:T(8,128)(2,1)}, u32[]{:S(2)}) copy-start(bf16[256,512]{1,0:T(8,128)(2,1)} %copy-done.15) | copy-start | bytes 786436
  344.6 24.7 %copy-start.8 = (bf16[256,512]{1,0:T(8,128)(2,1)S(1)}, bf16[256,512]{1,0:T(8,128)(2,1)}, u32[]{:S(2)}) copy-start(bf16[256,512]{1,0:T(8,128)(2,1)} %param.7) | copy-start | bytes 786436
  348.5 18.9 %all-to-all-start.7 = ((bf16[4,256,512]{2,1,0:T(8,128)(2,1)}), bf16[4,256,512]{2,1,0:T(8,128)(2,1)S(1)}, u32[]{:S(2)}, u32[]{:S(2)}) async-start(bf16[4,256,512]{2,1,0:T(8,128)(2,1)} %broadcast_in_dim.59), calls=%async_computation.8 | async-start | bytes 2097152 | tf_op jit(solution)/shard_map/all_to_all | solution.py:11
  353.8 100.5 %all-gather.5.cloned.1.call-start = ((), (), s32[]{:S(2)}) async-start(), calls=%async_computation.12 | async-start | bytes 3145728 | tf_op jit(solution)/shard_map/all_gather | solution.py:55
  (16 other events, 93.0 us)
Sparse Core Ops, SparseCore 0:
  10.7 54.5 all-gather.2
  228.2 76.3 reduce-scatter.4
  346.2 68.7 reduce-scatter.6
  416.4 37.8 all-gather.4
where the time goes:
time: 465 us; the launch traced here: 463 us
  waiting for transfers between devices  267 us (57%)
  other arithmetic  53.6 us (12%)
  matrix products  49 us (11%)
  starting transfers between devices  48.3 us (10%)
  local copies, waits for them, and re-layouts  30 us (6%)
  between operations  15.2 us (3%)
    all_to_all x8, waiting for transfers between devices, from_everyone(): return lax.all_to_all(copies, axis, split_axis=0, concat_axis=0, tiled=True)  111 us
    all_gather x1, waiting for transfers between devices, body(): columns = lax.all_gather(image_low, 'dp', axis=0, tiled=True)  52.9 us
    all_to_all x8, starting transfers between devices, from_everyone(): return lax.all_to_all(copies, axis, split_axis=0, concat_axis=0, tiled=True)  42.9 us
    unnamed x5, waiting for transfers between devices  42.6 us
    all_gather x1, waiting for transfers between devices, picked(): lax.all_gather(array, axis)  36.8 us
    dot_general x11, matrix products, contract_rows(): lax.dot_general(left_side, right_side, (((0,), (0,)), ((), ())), preferre...  25.3 us
    ppermute x4, waiting for transfers between devices, shifted(): return lax.ppermute(block, axis, route)  23.6 us
    dot_general x11, matrix products, contract_cols(): lax.dot_general(left_side, right_side, (((1,), (1,)), ((), ())), preferre...  16.1 us
  transfers between devices with their start and end apart: 16, of which 13 were waited for; matrix products, arithmetic and copies ran while one was open for 16% of the time, Pallas kernels for 0%

commit v1 on v0

v1 whole, which is shorter than its diff:
```python
import functools

import jax
import jax.numpy as jnp
from jax import lax
from jax.experimental import pallas as pl
from jax.experimental.pallas import tpu as pltpu
from jax.sharding import PartitionSpec as P

MESH = pl.DeviceIdType.MESH
F32 = jnp.float32
BF16 = jnp.bfloat16
LOW = -1e30


def dot_nt(a, b):
    return lax.dot_general(a, b, (((1,), (1,)), ((), ())), preferred_element_type=F32)


def dot_nn(a, b):
    return lax.dot_general(a, b, (((1,), (0,)), ((), ())), preferred_element_type=F32)


def dot_tn(a, b):
    return lax.dot_general(a, b, (((0,), (0,)), ((), ())), preferred_element_type=F32)


def unit_rows(values):
    wide = values.astype(F32)
    length = jnp.sqrt(jnp.sum(wide * wide, axis=1, keepdims=True) + 1.0)
    return wide / length, length


def unit_backward(unit, length, grad):
    return (grad - unit * jnp.sum(unit * grad, axis=1, keepdims=True)) / length


def slope_of(pre):
    s = jax.nn.sigmoid(1.702 * pre)
    return s + 1.702 * pre * s * (1.0 - s)


def rows(start, size=128):
    return pl.ds(pl.multiple_of(start, 128), size)


def copy_to(src, dst, send, recv, device):
    return pltpu.make_async_remote_copy(
        src_ref=src, dst_ref=dst, send_sem=send, recv_sem=recv, device_id=device, device_id_type=MESH
    )


def loop(count, fn, start=0):
    def step(i, _):
        fn(i)
        return 0

    lax.fori_loop(start, count, step, 0)


def kernel(
    scale, text, image, hin, win, wout,
    image_out, input_out, first_out, second_out,
    cols, tlow, tlow_t, scores, grads, row_m, row_s, row_a,
    rst, rst_in, rst_a, cst, cst_in, col_b,
    tshare, tshare_in, ishare, ishare_in, ihalf,
    wi_all, wo_all, hother, act, slope, slope_own, hin_t, gbuf, gin, gown, inbuf,
    wg1, wg1_in, wg2, wg2_in,
    cols_ss, cols_rs, wt_ss, wt_rs, h_s, rst_ss, rst_rs, cst_ss, cst_rs,
    ts_ss, ts_rs, is_ss, is_rs, ih_s, g1_ss, g0_ss, g_rs, in_ss, in_rs,
    w1_ss, w1_rs, w2_ss, w2_rs,
):
    section = lax.axis_index("section")
    dp = lax.axis_index("dp")
    mp = lax.axis_index("mp")
    me = section * 4 + mp
    x, core = me // 2, me % 2
    z, y = dp // 4, dp % 4
    mult = scale[0]

    def line(q):
        return {"section": q // 4, "mp": q % 4}

    def plane(k):
        return ((z + k // 4) % 4) * 4 + (y + k % 4) % 4

    def mirror(k):
        return ((4 - k // 4) % 4) * 4 + (4 - k % 4) % 4

    barrier = pltpu.get_barrier_semaphore()

    def greet_plane(k):
        pl.semaphore_signal(barrier, inc=1, device_id={"dp": plane(k)}, device_id_type=MESH)

    def greet_line(i):
        pl.semaphore_signal(barrier, inc=1, device_id=line((me + i) % 8), device_id_type=MESH)

    loop(16, greet_plane, 1)
    loop(8, greet_line, 1)

    own_half = image[pl.ds(pl.multiple_of(section * 128, 128), 128), :]
    image_unit, image_len = unit_rows(own_half)
    cols[0] = image_unit.astype(BF16)

    pl.semaphore_wait(barrier, 22)

    def cols_copy(k):
        return copy_to(cols.at[0], cols.at[mirror(k)], cols_ss.at[k], cols_rs.at[mirror(k)], {"dp": plane(k)})

    def cols_wait(k):
        copy_to(cols.at[k], cols.at[k], cols_ss.at[k], cols_rs.at[k], {"dp": dp}).wait_recv()

    loop(16, lambda k: cols_copy(k).start(), 1)

    right, left, opposite = (x + 1) % 4, (x + 3) % 4, (x + 2) % 4
    weights = (wi_all, wo_all)

    def weight_copy(n, origin, which, to, src=None):
        block = weights[which].at[origin]
        return copy_to(block if src is None else src, block, wt_ss.at[n], wt_rs.at[2 * origin + which], line(to))

    def weight_wait(origin, which):
        block = weights[which].at[origin]
        copy_to(block, block, wt_ss.at[0], wt_rs.at[2 * origin + which], line(me)).wait_recv()

    own_w = (win.at[0], wout.at[0])
    weight_plan = [
        (me, 0, right * 2 + core, own_w[0]),
        (me, 1, left * 2 + core, own_w[1]),
        (me, 1, right * 2 + core, own_w[1]),
        (me, 0, left * 2 + core, own_w[0]),
        (me, 0, x * 2 + 1 - core, own_w[0]),
        (me, 1, x * 2 + 1 - core, own_w[1]),
        (left * 2 + core, 0, right * 2 + core, None),
        (right * 2 + core, 1, left * 2 + core, None),
        (left * 2 + core, 0, x * 2 + 1 - core, None),
        (right * 2 + core, 1, x * 2 + 1 - core, None),
        (left * 2 + core, 1, x * 2 + 1 - core, None),
        (right * 2 + core, 0, x * 2 + 1 - core, None),
        (opposite * 2 + core, 0, x * 2 + 1 - core, None),
        (opposite * 2 + core, 1, x * 2 + 1 - core, None),
    ]

    def weight_send(n):
        origin, which, to, src = weight_plan[n]
        return weight_copy(n, origin, which, to, src)

    twin = (1 - section) * 4 + mp
    h_copy = copy_to(hin.at[0, rows(twin * 128), :], hother, h_s.at[0], h_s.at[1], line(twin))
    h_copy.start()
    for n in range(6):
        weight_send(n).start()

    def text_block(r):
        unit, _ = unit_rows(text[rows(r * 128), :])
        low = unit.astype(BF16)
        tlow[rows(r * 128), :] = low
        tlow_t[:, rows(r * 128)] = low.astype(F32).T.astype(BF16)
        row_m[rows(r * 128), :] = jnp.full((128, 128), LOW, F32)
        row_s[rows(r * 128), :] = jnp.zeros((128, 128), F32)

    loop(8, text_block)

    def score_pair(p):
        for j in (0, 1):
            pl.when(2 * p + j > 0)(functools.partial(cols_wait, 2 * p + j))
        pair = cols[pl.ds(2 * p, 2)].reshape(256, 512)
        scores[p] = dot_nt(tlow[...], pair) * mult

        def block(r, carry):
            c_m, c_s = carry
            s = scores[p, rows(r * 128), :]
            s3 = s.reshape(16, 8, 256)
            n_m = jnp.maximum(c_m, jnp.max(s3, axis=0))
            c_s = c_s * jnp.exp(c_m - n_m) + jnp.sum(jnp.exp(s3 - n_m[None]), axis=0)
            old = row_m[rows(r * 128), :]
            s0, s1 = s[:, :128], s[:, 128:]
            new = jnp.maximum(old, jnp.maximum(s0, s1))
            row_s[rows(r * 128), :] = (
                row_s[rows(r * 128), :] * jnp.exp(old - new) + jnp.exp(s0 - new) + jnp.exp(s1 - new)
            )
            row_m[rows(r * 128), :] = new
            return n_m, c_s

        c_m, c_s = lax.fori_loop(
            0, 8, block, (jnp.full((8, 256), LOW, F32), jnp.zeros((8, 256), F32))
        )
        peak = jnp.max(c_m, axis=0, keepdims=True)
        total = jnp.sum(c_s * jnp.exp(c_m - peak), axis=0, keepdims=True)
        for j in (0, 1):
            at = pl.ds(plane(2 * p + j), 1)
            cst[0, at, :] = peak[:, j * 128 : (j + 1) * 128]
            cst[1, at, :] = total[:, j * 128 : (j + 1) * 128]

    loop(8, score_pair)

    def cst_copy(k):
        return copy_to(cst, cst_in.at[dp], cst_ss.at[k], cst_rs.at[dp], {"dp": plane(k)})

    def cst_wait(k):
        copy_to(cst, cst_in.at[plane(k)], cst_ss.at[k], cst_rs.at[plane(k)], {"dp": dp}).wait_recv()

    loop(16, lambda k: cst_copy(k).start(), 1)
    cst_in[dp] = cst[...]

    for r in range(8):
        m_t = row_m[r * 128 : (r + 1) * 128, :].T
        s_t = row_s[r * 128 : (r + 1) * 128, :].T
        peak = jnp.max(m_t, axis=0, keepdims=True)
        rst[0, r : r + 1, :] = peak
        rst[1, r : r + 1, :] = jnp.sum(s_t * jnp.exp(m_t - peak), axis=0, keepdims=True)

    def rst_copy(i):
        q = (me + i) % 8
        return copy_to(rst, rst_in.at[me], rst_ss.at[i], rst_rs.at[me], line(q))

    def rst_wait(i):
        q = (me + i) % 8
        copy_to(rst, rst_in.at[q], rst_ss.at[i], rst_rs.at[q], line(me)).wait_recv()

    loop(8, lambda i: rst_copy(i).start(), 1)
    rst_in[me] = rst[...]

    weight_wait(left * 2 + core, 0)
    weight_send(6).start()
    weight_wait(right * 2 + core, 1)
    weight_send(7).start()
    weight_send(8).start()
    weight_send(9).start()

    def hidden_block(r):
        at = rows(r * 128)
        h = hin[0, at, :]
        pre = dot_nn(h, win[0])
        sig = jax.nn.sigmoid(1.702 * pre)
        act[at, :] = (pre * sig).astype(BF16)
        slope[at, :] = sig + 1.702 * pre * sig * (1.0 - sig)
        hin_t[:, at] = h.astype(F32).T.astype(BF16)

    loop(8, hidden_block)

    loop(8, rst_wait, 1)
    peak = jnp.max(rst_in[:, 0], axis=0)
    total = jnp.sum(rst_in[:, 1] * jnp.exp(rst_in[:, 0] - peak[None]), axis=0)
    rst_a[...] = peak + jnp.log(2.0 * total)
    for r in range(8):
        row_a[r * 128 : (r + 1) * 128, :] = jnp.broadcast_to(rst_a[r : r + 1, :], (128, 128)).T

    loop(16, cst_wait, 1)
    peak = jnp.max(cst_in[:, 0], axis=0)
    total = jnp.sum(cst_in[:, 1] * jnp.exp(cst_in[:, 0] - peak[None]), axis=0)
    col_b[...] = peak + jnp.log(2.0 * total)

    weight_wait(left * 2 + core, 1)
    weight_send(10).start()
    weight_wait(right * 2 + core, 0)
    weight_send(11).start()

    def prob(s, at, b):
        return jnp.exp(s - row_a[at, :]) + jnp.exp(s - b)

    def tshare_copy(q):
        return copy_to(tshare.at[q], tshare_in.at[me], ts_ss.at[q], ts_rs.at[me], line(q))

    def text_part(i):
        chip = (x + 1 + i) % 4

        def grad_block(t):
            p = t % 8
            at = rows(chip * 256 + (t // 8) * 128)
            for j in (0, 1):
                s = scores[p, at, j * 128 : (j + 1) * 128]
                b = col_b[pl.ds(plane(2 * p + j), 1), :]
                grads[at, pl.ds(pl.multiple_of(p * 256 + j * 128, 128), 128)] = prob(s, at, b).astype(BF16)

        loop(16, grad_block)

        mine = 2 * mp + section

        @pl.when(mine // 2 == chip)
        def _():
            at = rows(mine * 128)
            s = scores[0, at, :128]
            eye = lax.broadcasted_iota(jnp.int32, (128, 128), 0) == lax.broadcasted_iota(jnp.int32, (128, 128), 1)
            part = prob(s, at, col_b[pl.ds(dp, 1), :])
            grads[at, :128] = (part - jnp.where(eye, 1.0, 0.0)).astype(BF16)

        part = dot_nn(grads[rows(chip * 256, 256), :], cols[...].reshape(2048, 512))
        for j in (0, 1):
            q = chip * 2 + j
            tshare[q] = part[j * 128 : (j + 1) * 128].astype(BF16)
            pl.when(q != me)(lambda q=q: tshare_copy(q).start())

    loop(4, text_part)

    def ishare_copy(k):
        return copy_to(ishare.at[k], ishare_in.at[mirror(k)], is_ss.at[k], is_rs.at[mirror(k)], {"dp": plane(k)})

    def image_part(p):
        part = dot_nn(tlow_t[...], grads[:, pl.ds(pl.multiple_of(p * 256, 256), 256)])
        for j in (0, 1):
            k = 2 * p + j
            ishare[k] = part[:, j * 128 : (j + 1) * 128].astype(BF16)
            pl.when(k > 0)(lambda k=k: ishare_copy(k).start())

    loop(8, image_part)

    weight_wait(opposite * 2 + core, 0)
    weight_send(12).start()
    weight_wait(opposite * 2 + core, 1)
    weight_send(13).start()

    h_copy.wait_recv()

    def own_block(r):
        def other_wait():
            for which in (0, 1):
                weight_wait(r, which)

        pl.when(r % 2 != core)(other_wait)

        @pl.when(r == me)
        def _():
            wi_all[r] = win[0]
            wo_all[r] = wout[0]

        h = jnp.where(r // 4 == section, hin[0, rows(me * 128), :], hother[...])
        slope_own[r] = slope_of(dot_nn(h, wi_all[r]))

    loop(8, own_block)

    def tshare_sum(i, acc):
        q = (me + i) % 8
        copy_to(tshare.at[q], tshare_in.at[q], ts_ss.at[q], ts_rs.at[q], line(me)).wait_recv()
        return acc + tshare_in[q].astype(F32)

    total = lax.fori_loop(1, 8, tshare_sum, tshare[me].astype(F32)) * mult
    unit, length = unit_rows(text[rows(me * 128), :])
    gown[0] = unit_backward(unit, length, total).astype(BF16)

    def g_copy(layer, m, sems):
        return copy_to(gown.at[1 - layer], gbuf.at[me], sems.at[m], g_rs.at[me], {"section": layer, "mp": m})

    def g_send(layer, sems):
        for m in range(4):
            pl.when(me != layer * 4 + m)(lambda m=m: g_copy(layer, m, sems).start())

        @pl.when(section == layer)
        def _():
            gbuf[me] = gown[1 - layer]

    def chain(layer):
        g = gown[1 - layer]

        def step(j, acc):
            q = layer * 4 + j
            back = dot_nt(g, wo_all[q])
            pre_grad = (back * slope_own[q]).astype(BF16)
            return acc + dot_nt(pre_grad, wi_all[q])

        return lax.fori_loop(0, 4, step, g.astype(F32)).astype(BF16)

    g_send(1, g1_ss)
    gown[1] = chain(1)
    g_send(0, g0_ss)
    lowest = chain(0)
    gin[0] = lowest[:, :256]
    gin[1] = lowest[:, 256:]

    def in_copy(i):
        q = (me + i) % 8
        return copy_to(gin.at[q // 4], inbuf.at[me], in_ss.at[i], in_rs.at[me], line(q))

    loop(8, lambda i: in_copy(i).start(), 1)
    inbuf[me] = gin[section]

    def g_wait(i):
        q = (me + i) % 8
        copy_to(gbuf.at[q], gbuf.at[q], g1_ss.at[0], g_rs.at[q], line(me)).wait_recv()

    loop(8, g_wait, 1)

    full = gbuf[...].reshape(1024, 512)

    def wg_copy(buf, landed, ss, rs, k):
        return copy_to(buf.at[plane(k)], landed.at[dp], ss.at[k], rs.at[dp], {"dp": plane(k)})

    wg2[...] = dot_tn(full, act[...]).reshape(16, 32, 512).astype(BF16)
    loop(16, lambda k: wg_copy(wg2, wg2_in, w2_ss, w2_rs, k).start(), 1)

    def back_block(r):
        at = rows(r * 128)
        back = dot_nt(gbuf[r], wout[0])
        act[at, :] = (back * slope[at, :]).astype(BF16)

    loop(8, back_block)
    wg1[...] = dot_nn(hin_t[...], act[...]).reshape(16, 32, 512).astype(BF16)
    loop(16, lambda k: wg_copy(wg1, wg1_in, w1_ss, w1_rs, k).start(), 1)

    def ishare_sum(k, acc):
        copy_to(ishare.at[k], ishare_in.at[k], is_ss.at[k], is_rs.at[k], {"dp": dp}).wait_recv()
        return acc + ishare_in[k].astype(F32)

    total = lax.fori_loop(1, 16, ishare_sum, ishare[0].astype(F32)).T * mult
    own_half = image[pl.ds(pl.multiple_of(section * 128, 128), 128), :]
    image_unit, image_len = unit_rows(own_half)
    ihalf[0] = unit_backward(image_unit, image_len, total).astype(BF16)
    ihalf_copy = copy_to(ihalf.at[0], ihalf.at[1], ih_s.at[0], ih_s.at[1], line(twin))
    ihalf_copy.start()

    def in_wait(i):
        q = (me + i) % 8
        copy_to(gin.at[0], inbuf.at[q], in_ss.at[i], in_rs.at[q], line(me)).wait_recv()

    loop(8, in_wait, 1)
    input_out[...] = inbuf[...].reshape(1024, 256)

    def wg_sum(buf, landed, ss, rs, out):
        def step(k, acc):
            copy_to(buf.at[0], landed.at[plane(k)], ss.at[k], rs.at[plane(k)], {"dp": dp}).wait_recv()
            return acc + landed[plane(k)].astype(F32)

        out[0] = lax.fori_loop(1, 16, step, buf[dp].astype(F32))

    image_out[rows(section * 128), :] = ihalf[0]
    ihalf_copy.wait_recv()
    image_out[rows((1 - section) * 128), :] = ihalf[1]
    wg_sum(wg2, wg2_in, w2_ss, w2_rs, second_out)
    wg_sum(wg1, wg1_in, w1_ss, w1_rs, first_out)

    loop(16, lambda k: cols_copy(k).wait_send(), 1)
    h_copy.wait_send()
    for n in range(14):
        weight_send(n).wait_send()
    loop(16, lambda k: cst_copy(k).wait_send(), 1)
    loop(8, lambda i: rst_copy(i).wait_send(), 1)
    loop(8, lambda i: tshare_copy((me + i) % 8).wait_send(), 1)
    loop(16, lambda k: ishare_copy(k).wait_send(), 1)
    ihalf_copy.wait_send()
    for layer, sems in ((1, g1_ss), (0, g0_ss)):
        for m in range(4):
            pl.when(me != layer * 4 + m)(lambda m=m, layer=layer, sems=sems: g_copy(layer, m, sems).wait_send())
    loop(8, lambda i: in_copy(i).wait_send(), 1)
    loop(16, lambda k: wg_copy(wg2, wg2_in, w2_ss, w2_rs, k).wait_send(), 1)
    loop(16, lambda k: wg_copy(wg1, wg1_in, w1_ss, w1_rs, k).wait_send(), 1)


def body(text_feats, image_feats, logit_scale, layer_inputs, w_in, w_out):
    vmem = pl.BlockSpec(memory_space=pltpu.VMEM)
    dma = pltpu.SemaphoreType.DMA
    scratch = [
        pltpu.VMEM((16, 128, 512), BF16),
        pltpu.VMEM((1024, 512), BF16),
        pltpu.VMEM((512, 1024), BF16),
        pltpu.VMEM((8, 1024, 256), F32),
        pltpu.VMEM((1024, 2048), BF16),
        pltpu.VMEM((1024, 128), F32),
        pltpu.VMEM((1024, 128), F32),
        pltpu.VMEM((1024, 128), F32),
        pltpu.VMEM((2, 8, 128), F32),
        pltpu.VMEM((8, 2, 8, 128), F32),
        pltpu.VMEM((8, 128), F32),
        pltpu.VMEM((2, 16, 128), F32),
        pltpu.VMEM((16, 2, 16, 128), F32),
        pltpu.VMEM((16, 128), F32),
        pltpu.VMEM((8, 128, 512), BF16),
        pltpu.VMEM((8, 128, 512), BF16),
        pltpu.VMEM((16, 512, 128), BF16),
        pltpu.VMEM((16, 512, 128), BF16),
        pltpu.VMEM((2, 128, 512), BF16),
        pltpu.VMEM((8, 512, 512), BF16),
        pltpu.VMEM((8, 512, 512), BF16),
        pltpu.VMEM((128, 512), BF16),
        pltpu.VMEM((1024, 512), BF16),
        pltpu.VMEM((1024, 512), F32),
        pltpu.VMEM((8, 128, 512), F32),
        pltpu.VMEM((512, 1024), BF16),
        pltpu.VMEM((8, 128, 512), BF16),
        pltpu.VMEM((2, 128, 256), BF16),
        pltpu.VMEM((2, 128, 512), BF16),
        pltpu.VMEM((8, 128, 256), BF16),
        pltpu.VMEM((16, 32, 512), BF16),
        pltpu.VMEM((16, 32, 512), BF16),
        pltpu.VMEM((16, 32, 512), BF16),
        pltpu.VMEM((16, 32, 512), BF16),
        dma((16,)), dma((16,)),
        dma((14,)), dma((16,)),
        dma((2,)),
        dma((8,)), dma((8,)),
        dma((16,)), dma((16,)),
        dma((8,)), dma((8,)),
        dma((16,)), dma((16,)),
        dma((2,)),
        dma((4,)), dma((4,)), dma((8,)),
        dma((8,)), dma((8,)),
        dma((16,)), dma((16,)), dma((16,)), dma((16,)),
    ]
    return pl.pallas_call(
        kernel,
        out_shape=(
            jax.ShapeDtypeStruct((256, 512), BF16),
            jax.ShapeDtypeStruct((1024, 256), BF16),
            jax.ShapeDtypeStruct((1, 32, 512), F32),
            jax.ShapeDtypeStruct((1, 32, 512), F32),
        ),
        in_specs=[pl.BlockSpec(memory_space=pltpu.SMEM)] + [vmem] * 5,
        out_specs=(vmem,) * 4,
        scratch_shapes=scratch,
        compiler_params=pltpu.CompilerParams(
            collective_id=0, has_side_effects=True, vmem_limit_bytes=62 * 1024 * 1024
        ),
    )(logit_scale, text_feats, image_feats, layer_inputs, w_in, w_out)


def solution(mesh):
    placed = (
        P("dp", None),
        P(("dp", "mp"), None),
        P(),
        P("section", "dp", None),
        P("section", None, "mp"),
        P("section", "mp", None),
    )
    return jax.shard_map(
        body,
        mesh=mesh,
        in_specs=placed,
        out_specs=(
            P(("dp", "mp"), None),
            P("dp", "section"),
            P("section", "dp", "mp"),
            P("section", "dp", "mp"),
        ),
        check_vma=False,
    )
```

time: 465 us -> 115 us (0.25)
  waiting for transfers between devices: 267 us -> 0 us
  Pallas kernels: 0 us -> 109 us
  other arithmetic: 53.6 us -> 0 us
  matrix products: 49 us -> 0 us
  starting transfers between devices: 48.3 us -> 0 us
  local copies, waits for them, and re-layouts: 30 us -> 4.08 us
  between operations: 15.2 us -> 1.3 us
    all_to_all x8 -> x0, waiting for transfers between devices: 111 us -> none  [from_everyone(): return lax.all_to_all(copies, axis, split_axis=0, concat_axis=0, tiled=True)]
    pallas_call x0 -> x1, Pallas kernels: none -> 109 us  [body(): pl.pallas_call(kernel, out_shape=(jax.ShapeDtypeStruct((256, 512), BF16),...]
    all_gather x2 -> x0, waiting for transfers between devices: 89.7 us -> none  [the longest x1 52.9 us: body(): columns = lax.all_gather(image_low, 'dp', axis=0, tiled=True)]
    dot_general x28 -> x0, matrix products: 49 us -> none  [the longest x11 25.3 us: contract_rows(): lax.dot_general(left_side, right_side, (((0,), (0,)), ((), ())), preferre...]
    all_to_all x8 -> x0, starting transfers between devices: 42.9 us -> none  [from_everyone(): return lax.all_to_all(copies, axis, split_axis=0, concat_axis=0, tiled=True)]
    unnamed x5 -> x0, waiting for transfers between devices: 42.6 us -> none
    reduce_sum x12 -> x0, other arithmetic: 26.4 us -> none  [the longest x6 9.19 us: of_everyone(): return from_everyone(array, axis).astype(jnp.float32).sum(axis=0)]
    ppermute x4 -> x0, waiting for transfers between devices: 23.6 us -> none  [shifted(): return lax.ppermute(block, axis, route)]
  transfers between devices with their start and end apart: 16 -> 0, of which waited for: 13 -> 0; matrix products, arithmetic and copies ran while one was open for 16% -> 0% of each run, Pallas kernels for 0% -> 0%
where the time goes in v1:
time: 115 us; the launch traced here: 114 us
  Pallas kernels  109 us (95%)
  local copies, waits for them, and re-layouts  4.08 us (4%)
  between operations  1.3 us (1%)
    pallas_call x1, Pallas kernels, body(): pl.pallas_call(kernel, out_shape=(jax.ShapeDtypeStruct((256, 512), BF16),...  109 us
    unnamed x10, local copies, waits for them, and re-layouts  4.08 us

profile of v1, /device:TPU:1, one launch (start us, length us, event | category | flops | bytes accessed | tf_op | source)
XLA Modules:
  0.0 114.5 jit_solution(10373094609781329190)
XLA Ops:
  1.3 109.1 %shard_map.93 = (bf16[256,512]{1,0:T(8,128)(2,1)}, bf16[1024,256]{1,0:T(8,128)(2,1)}, f32[1,32,512]{2,1,0:T(8,128)}, f32[1,32,512]{2,1,0:T(8,128)}) custom-call(f32[1]{0:T(128)S(6)} %copy.14.scale, bf16[1024,512]{1,0:T(8,128)(2,1)} %text.1, bf16[256,512]{1,0:T(8,128)(2,1)} %image.1, bf16[1,1024,512]{2,1,0:T(8,128)(2,1)} %hin.1, bf16[1,512,512]{2,1,0:T(8,128)(2,1)} %win.1, ...), custom_call_target="tpu_custom_call" | custom-call | tf_op jit(solution)/shard_map/pallas_call | solution.py:498
  110.4 0.0 copy-start
  110.4 1.7 %copy.15 = bf16[256,512]{1,0:T(8,128)(2,1)} copy(bf16[256,512]{1,0:T(8,128)(2,1)} %get-tuple-element.8) | data formatting | bytes 524288
  112.1 0.0 copy-done
  112.1 0.0 copy-start.2
  112.1 0.8 copy.16
  112.9 0.1 copy-done.2
  113.0 0.0 copy-start.1
  113.0 0.6 copy.17
  113.6 0.2 copy-done.1
  113.9 0.6 copy.18
Async XLA Ops:
  110.4 1.7 %copy-start = (bf16[1024,256]{1,0:T(8,128)(2,1)S(1)}, bf16[1024,256]{1,0:T(8,128)(2,1)}, u32[]{:S(2)}) copy-start(bf16[1024,256]{1,0:T(8,128)(2,1)} %get-tuple-element.9) | copy-start | bytes 1572868
  112.1 0.9 copy-start.2
  113.0 0.9 copy-start.1

commit v2 on v1

--- a/solution.py
+++ b/solution.py
@@ -11,6 +11,10 @@
 F32 = jnp.float32
 BF16 = jnp.bfloat16
 LOW = -1e30
+ORDER = (
+    (0, 0), (0, 1), (0, 3), (1, 0), (3, 0), (1, 1), (1, 3), (3, 1),
+    (3, 3), (0, 2), (2, 0), (1, 2), (3, 2), (2, 1), (2, 3), (2, 2),
+)
 
 
 def dot_nt(a, b):
@@ -62,12 +66,13 @@
     scale, text, image, hin, win, wout,
     image_out, input_out, first_out, second_out,
     cols, tlow, tlow_t, scores, grads, row_m, row_s, row_a,
-    rst, rst_in, rst_a, cst, cst_in, col_b,
-    tshare, tshare_in, ishare, ishare_in, ihalf,
+    rst, rst_in, rst_a, own_stat, cst, cst_in, col_b,
+    tshare, tpass, tshare_in, ishare, ifar_in, isum, inear_in, ifull, ihalf,
     wi_all, wo_all, hother, act, slope, slope_own, hin_t, gbuf, gin, gown, inbuf,
     wg1, wg1_in, wg2, wg2_in,
     cols_ss, cols_rs, wt_ss, wt_rs, h_s, rst_ss, rst_rs, cst_ss, cst_rs,
-    ts_ss, ts_rs, is_ss, is_rs, ih_s, g1_ss, g0_ss, g_rs, in_ss, in_rs,
+    tp_ss, tp_rs, ts_ss, ts_rs, if_ss, if_rs, ir_ss, ir_rs, ih_s,
+    g1_ss, g0_ss, gp_ss, g_rs, in_ss, in_rs,
     w1_ss, w1_rs, w2_ss, w2_rs,
 ):
     section = lax.axis_index("section")
@@ -81,16 +86,21 @@
     def line(q):
         return {"section": q // 4, "mp": q % 4}
 
-    def plane(k):
-        return ((z + k // 4) % 4) * 4 + (y + k % 4) % 4
-
-    def mirror(k):
-        return ((4 - k // 4) % 4) * 4 + (4 - k % 4) % 4
+    def plane(dz, dy):
+        return ((z + dz) % 4) * 4 + (y + dy) % 4
+
+    def slot(dz, dy):
+        return ORDER.index((dz % 4, dy % 4))
+
+    def away(k):
+        return plane(k // 4, k % 4)
+
+    sends = []
 
     barrier = pltpu.get_barrier_semaphore()
 
     def greet_plane(k):
-        pl.semaphore_signal(barrier, inc=1, device_id={"dp": plane(k)}, device_id_type=MESH)
+        pl.semaphore_signal(barrier, inc=1, device_id={"dp": away(k)}, device_id_type=MESH)
 
     def greet_line(i):
         pl.semaphore_signal(barrier, inc=1, device_id=line((me + i) % 8), device_id_type=MESH)
@@ -102,15 +112,49 @@
     image_unit, image_len = unit_rows(own_half)
     cols[0] = image_unit.astype(BF16)
 
+    def text_block(r):
+        unit, _ = unit_rows(text[rows(r * 128), :])
+        low = unit.astype(BF16)
+        tlow[rows(r * 128), :] = low
+        tlow_t[:, rows(r * 128)] = low.astype(F32).T.astype(BF16)
+        row_m[rows(r * 128), :] = jnp.full((128, 128), LOW, F32)
+        row_s[rows(r * 128), :] = jnp.zeros((128, 128), F32)
+
+    loop(8, text_block)
     pl.semaphore_wait(barrier, 22)
 
-    def cols_copy(k):
-        return copy_to(cols.at[0], cols.at[mirror(k)], cols_ss.at[k], cols_rs.at[mirror(k)], {"dp": plane(k)})
-
-    def cols_wait(k):
-        copy_to(cols.at[k], cols.at[k], cols_ss.at[k], cols_rs.at[k], {"dp": dp}).wait_recv()
-
-    loop(16, lambda k: cols_copy(k).start(), 1)
+    def ag_send(dz, dy, lo, size, ez, ey):
+        there = slot(dz - ez, dy - ey)
+        copy = copy_to(
+            cols.at[slot(dz, dy), lo : lo + size],
+            cols.at[there, lo : lo + size],
+            cols_ss.at[len(sends)],
+            cols_rs.at[there * 4 + lo // 32],
+            {"dp": plane(ez, ey)},
+        )
+        copy.start()
+        sends.append(copy)
+
+    def ag_wait(dz, dy, lo, size):
+        here = slot(dz, dy)
+        block = cols.at[here, lo : lo + size]
+        copy_to(block, block, cols_ss.at[0], cols_rs.at[here * 4 + lo // 32], {"dp": dp}).wait_recv()
+
+    def flip(swap, *pair):
+        return pair[::-1] if swap else pair
+
+    def half_send(swap, first, second, to_first, to_second, lo=0, size=64):
+        dz, dy = flip(swap, first, second)
+        ez, ey = flip(swap, to_first, to_second)
+        ag_send(dz, dy, lo + 64 * swap, size, ez, ey)
+
+    def half_wait(swap, first, second, lo=0, size=64):
+        dz, dy = flip(swap, first, second)
+        ag_wait(dz, dy, lo + 64 * swap, size)
+
+    for to in ((0, 1), (0, 3), (1, 0), (3, 0)):
+        for swap in (0, 1):
+            half_send(swap, 0, 0, *to)
 
     right, left, opposite = (x + 1) % 4, (x + 3) % 4, (x + 2) % 4
     weights = (wi_all, wo_all)
@@ -151,19 +195,7 @@
     for n in range(6):
         weight_send(n).start()
 
-    def text_block(r):
-        unit, _ = unit_rows(text[rows(r * 128), :])
-        low = unit.astype(BF16)
-        tlow[rows(r * 128), :] = low
-        tlow_t[:, rows(r * 128)] = low.astype(F32).T.astype(BF16)
-        row_m[rows(r * 128), :] = jnp.full((128, 128), LOW, F32)
-        row_s[rows(r * 128), :] = jnp.zeros((128, 128), F32)
-
-    loop(8, text_block)
-
     def score_pair(p):
-        for j in (0, 1):
-            pl.when(2 * p + j > 0)(functools.partial(cols_wait, 2 * p + j))
         pair = cols[pl.ds(2 * p, 2)].reshape(256, 512)
         scores[p] = dot_nt(tlow[...], pair) * mult
 
@@ -188,17 +220,57 @@
         peak = jnp.max(c_m, axis=0, keepdims=True)
         total = jnp.sum(c_s * jnp.exp(c_m - peak), axis=0, keepdims=True)
         for j in (0, 1):
-            at = pl.ds(plane(2 * p + j), 1)
-            cst[0, at, :] = peak[:, j * 128 : (j + 1) * 128]
-            cst[1, at, :] = total[:, j * 128 : (j + 1) * 128]
-
-    loop(8, score_pair)
+            own_stat[0, pl.ds(2 * p + j, 1), :] = peak[:, j * 128 : (j + 1) * 128]
+            own_stat[1, pl.ds(2 * p + j, 1), :] = total[:, j * 128 : (j + 1) * 128]
+
+    def spread(swap, first, second):
+        for to in (1, 3):
+            half_send(swap, first, second, to, 0)
+
+    both = (0, 1)
+    for swap in both:
+        half_wait(swap, 0, 1)
+        half_wait(swap, 0, 3)
+        half_send(swap, 0, 1, 0, 3, 0, 32)
+        half_send(swap, 0, 3, 0, 1, 32, 32)
+    for swap in both:
+        spread(swap, 0, 1)
+        spread(swap, 0, 3)
+    for swap in both:
+        half_wait(swap, 1, 0)
+        half_send(swap, 1, 0, 3, 0)
+        half_wait(swap, 3, 0)
+    for swap in both:
+        half_wait(swap, 0, 2, 0, 32)
+        half_wait(swap, 0, 2, 32, 32)
+        spread(swap, 0, 2)
+    loop(2, score_pair)
+    for swap in both:
+        for second in (1, 3):
+            half_wait(swap, 3, second)
+            half_send(swap, 3, second, 1, 0)
+            half_wait(swap, 1, second)
+        half_wait(swap, 2, 0)
+    loop(5, score_pair, 2)
+    for swap in both:
+        half_wait(swap, 1, 2)
+        half_send(swap, 1, 2, 3, 0)
+        half_wait(swap, 3, 2)
+    for swap in both:
+        half_wait(swap, 2, 1)
+        half_wait(swap, 2, 3)
+    loop(7, score_pair, 5)
+    for swap in both:
+        half_wait(swap, 2, 2)
+    score_pair(7)
+    for k, (dz, dy) in enumerate(ORDER):
+        cst[:, pl.ds(plane(dz, dy), 1), :] = own_stat[:, k : k + 1, :]
 
     def cst_copy(k):
-        return copy_to(cst, cst_in.at[dp], cst_ss.at[k], cst_rs.at[dp], {"dp": plane(k)})
+        return copy_to(cst, cst_in.at[dp], cst_ss.at[k], cst_rs.at[dp], {"dp": away(k)})
 
     def cst_wait(k):
-        copy_to(cst, cst_in.at[plane(k)], cst_ss.at[k], cst_rs.at[plane(k)], {"dp": dp}).wait_recv()
+        copy_to(cst, cst_in.at[away(k)], cst_ss.at[k], cst_rs.at[away(k)], {"dp": dp}).wait_recv()
 
     loop(16, lambda k: cst_copy(k).start(), 1)
     cst_in[dp] = cst[...]
@@ -249,7 +321,9 @@
     loop(16, cst_wait, 1)
     peak = jnp.max(cst_in[:, 0], axis=0)
     total = jnp.sum(cst_in[:, 1] * jnp.exp(cst_in[:, 0] - peak[None]), axis=0)
-    col_b[...] = peak + jnp.log(2.0 * total)
+    cst_in[dp, 0] = peak + jnp.log(2.0 * total)
+    for k, (dz, dy) in enumerate(ORDER):
+        col_b[k : k + 1, :] = cst_in[dp, 0, pl.ds(plane(dz, dy), 1), :]
 
     weight_wait(left * 2 + core, 1)
     weight_send(10).start()
@@ -259,18 +333,21 @@
     def prob(s, at, b):
         return jnp.exp(s - row_a[at, :]) + jnp.exp(s - b)
 
-    def tshare_copy(q):
-        return copy_to(tshare.at[q], tshare_in.at[me], ts_ss.at[q], ts_rs.at[me], line(q))
-
-    def text_part(i):
-        chip = (x + 1 + i) % 4
-
+    def pass_copy(chip):
+        other = chip * 2 + 1 - core
+        return copy_to(tshare.at[other], tpass.at[chip], tp_ss.at[chip], tp_rs.at[chip], line(x * 2 + 1 - core))
+
+    def tshare_copy(chip):
+        own = chip * 2 + core
+        return copy_to(tshare.at[own], tshare_in.at[x], ts_ss.at[chip], ts_rs.at[x], line(own))
+
+    def text_part(chip):
         def grad_block(t):
             p = t % 8
             at = rows(chip * 256 + (t // 8) * 128)
             for j in (0, 1):
                 s = scores[p, at, j * 128 : (j + 1) * 128]
-                b = col_b[pl.ds(plane(2 * p + j), 1), :]
+                b = col_b[pl.ds(2 * p + j, 1), :]
                 grads[at, pl.ds(pl.multiple_of(p * 256 + j * 128, 128), 128)] = prob(s, at, b).astype(BF16)
 
         loop(16, grad_block)
@@ -282,28 +359,56 @@
             at = rows(mine * 128)
             s = scores[0, at, :128]
             eye = lax.broadcasted_iota(jnp.int32, (128, 128), 0) == lax.broadcasted_iota(jnp.int32, (128, 128), 1)
-            part = prob(s, at, col_b[pl.ds(dp, 1), :])
+            part = prob(s, at, col_b[0:1, :])
             grads[at, :128] = (part - jnp.where(eye, 1.0, 0.0)).astype(BF16)
 
         part = dot_nn(grads[rows(chip * 256, 256), :], cols[...].reshape(2048, 512))
         for j in (0, 1):
-            q = chip * 2 + j
-            tshare[q] = part[j * 128 : (j + 1) * 128].astype(BF16)
-            pl.when(q != me)(lambda q=q: tshare_copy(q).start())
-
-    loop(4, text_part)
-
-    def ishare_copy(k):
-        return copy_to(ishare.at[k], ishare_in.at[mirror(k)], is_ss.at[k], is_rs.at[mirror(k)], {"dp": plane(k)})
+            tshare[chip * 2 + j] = part[j * 128 : (j + 1) * 128].astype(BF16)
+        pass_copy(chip).start()
+
+    def text_merge(chip):
+        own = chip * 2 + core
+        pass_copy(chip).wait_recv()
+        tshare[own] = (tshare[own].astype(F32) + tpass[chip].astype(F32)).astype(BF16)
+
+    def text_step(i):
+        chip = jnp.where(i == 0, opposite, jnp.where(i == 1, right, jnp.where(i == 2, left, x)))
+        last = jnp.where(i == 1, opposite, jnp.where(i == 2, right, left))
+        text_part(chip)
+
+        @pl.when(i > 0)
+        def _():
+            text_merge(last)
+            tshare_copy(last).start()
+
+    loop(4, text_step)
+    text_merge(x)
 
     def image_part(p):
-        part = dot_nn(tlow_t[...], grads[:, pl.ds(pl.multiple_of(p * 256, 256), 256)])
+        part = dot_nn(tlow_t[...], grads[:, p * 256 : (p + 1) * 256])
         for j in (0, 1):
-            k = 2 * p + j
-            ishare[k] = part[:, j * 128 : (j + 1) * 128].astype(BF16)
-            pl.when(k > 0)(lambda k=k: ishare_copy(k).start())
-
-    loop(8, image_part)
+            dz, dy = ORDER[2 * p + j]
+            block = part[:, j * 128 : (j + 1) * 128].astype(BF16)
+            ishare[0, dz, dy] = block[:256]
+            ishare[1, dy, dz] = block[256:]
+
+    def step_of(swap, far):
+        return {"dp": plane(*flip(swap, far, 0))}
+
+    def image_far(swap, far):
+        n = swap * 3 + 3 - far
+        return copy_to(ishare.at[swap, far], ifar_in.at[swap, 3 - far], if_ss.at[n], if_rs.at[n], step_of(swap, far))
+
+    def image_near(swap, far):
+        n = swap * 3 + 3 - far
+        return copy_to(isum.at[swap, far], inear_in.at[swap, 3 - far], ir_ss.at[n], ir_rs.at[n], step_of(1 - swap, far))
+
+    for p in range(7, -1, -1):
+        image_part(p)
+    for far in (2, 1, 3):
+        for swap in both:
+            image_far(swap, far).start()
 
     weight_wait(opposite * 2 + core, 0)
     weight_send(12).start()
@@ -330,24 +435,36 @@
     loop(8, own_block)
 
     def tshare_sum(i, acc):
-        q = (me + i) % 8
-        copy_to(tshare.at[q], tshare_in.at[q], ts_ss.at[q], ts_rs.at[q], line(me)).wait_recv()
-        return acc + tshare_in[q].astype(F32)
-
-    total = lax.fori_loop(1, 8, tshare_sum, tshare[me].astype(F32)) * mult
+        chip = (x + i) % 4
+        copy_to(tshare.at[0], tshare_in.at[chip], ts_ss.at[chip], ts_rs.at[chip], line(me)).wait_recv()
+        return acc + tshare_in[chip].astype(F32)
+
+    total = lax.fori_loop(1, 4, tshare_sum, tshare[me].astype(F32)) * mult
     unit, length = unit_rows(text[rows(me * 128), :])
     gown[0] = unit_backward(unit, length, total).astype(BF16)
 
-    def g_copy(layer, m, sems):
-        return copy_to(gown.at[1 - layer], gbuf.at[me], sems.at[m], g_rs.at[me], {"section": layer, "mp": m})
+    def g_copy(layer, lo, sems):
+        to = {"section": layer, "mp": lo * 2 + core}
+        return copy_to(gown.at[1 - layer], gbuf.at[me], sems.at[lo], g_rs.at[me], to)
 
     def g_send(layer, sems):
-        for m in range(4):
-            pl.when(me != layer * 4 + m)(lambda m=m: g_copy(layer, m, sems).start())
+        for lo in (0, 1):
+            pl.when(x != layer * 2 + lo)(lambda lo=lo: g_copy(layer, lo, sems).start())
 
         @pl.when(section == layer)
         def _():
             gbuf[me] = gown[1 - layer]
+
+    def g_pass(i):
+        q = ((x + i) % 4) * 2 + core
+        return copy_to(gbuf.at[q], gbuf.at[q], gp_ss.at[i], g_rs.at[q], line(x * 2 + 1 - core))
+
+    def g_arrive(q):
+        copy_to(gbuf.at[q], gbuf.at[q], gp_ss.at[0], g_rs.at[q], line(me)).wait_recv()
+
+    def g_relay(i):
+        g_arrive(((x + i) % 4) * 2 + core)
+        g_pass(i).start()
 
     def chain(layer):
         g = gown[1 - layer]
@@ -371,19 +488,28 @@
         q = (me + i) % 8
         return copy_to(gin.at[q // 4], inbuf.at[me], in_ss.at[i], in_rs.at[me], line(q))
 
+    def image_fold(swap):
+        total = ishare[swap, 0].astype(F32)
+        for far in (1, 2, 3):
+            landed = ifar_in.at[swap, far - 1]
+            copy_to(landed, landed, if_ss.at[0], if_rs.at[swap * 3 + far - 1], {"dp": dp}).wait_recv()
+            total = total + landed[...].astype(F32)
+        isum[swap] = total.astype(BF16)
+        for far in (2, 1, 3):
+            image_near(swap, far).start()
+
+    for swap in both:
+        image_fold(swap)
+    g_pass(0).start()
+    loop(4, g_relay, 1)
     loop(8, lambda i: in_copy(i).start(), 1)
     inbuf[me] = gin[section]
-
-    def g_wait(i):
-        q = (me + i) % 8
-        copy_to(gbuf.at[q], gbuf.at[q], g1_ss.at[0], g_rs.at[q], line(me)).wait_recv()
-
-    loop(8, g_wait, 1)
+    loop(4, lambda i: g_arrive(((x + i) % 4) * 2 + 1 - core))
 
     full = gbuf[...].reshape(1024, 512)
 
     def wg_copy(buf, landed, ss, rs, k):
-        return copy_to(buf.at[plane(k)], landed.at[dp], ss.at[k], rs.at[dp], {"dp": plane(k)})
+        return copy_to(buf.at[away(k)], landed.at[dp], ss.at[k], rs.at[dp], {"dp": away(k)})
 
     wg2[...] = dot_tn(full, act[...]).reshape(16, 32, 512).astype(BF16)
     loop(16, lambda k: wg_copy(wg2, wg2_in, w2_ss, w2_rs, k).start(), 1)
@@ -397,11 +523,14 @@
     wg1[...] = dot_nn(hin_t[...], act[...]).reshape(16, 32, 512).astype(BF16)
     loop(16, lambda k: wg_copy(wg1, wg1_in, w1_ss, w1_rs, k).start(), 1)
 
-    def ishare_sum(k, acc):
-        copy_to(ishare.at[k], ishare_in.at[k], is_ss.at[k], is_rs.at[k], {"dp": dp}).wait_recv()
-        return acc + ishare_in[k].astype(F32)
-
-    total = lax.fori_loop(1, 16, ishare_sum, ishare[0].astype(F32)).T * mult
+    for swap in both:
+        total = isum[swap, 0].astype(F32)
+        for far in (1, 2, 3):
+            landed = inear_in.at[swap, far - 1]
+            copy_to(landed, landed, ir_ss.at[0], ir_rs.at[swap * 3 + far - 1], {"dp": dp}).wait_recv()
+            total = total + landed[...].astype(F32)
+        ifull[:, swap * 256 : (swap + 1) * 256] = total.T
+    total = ifull[...] * mult
     own_half = image[pl.ds(pl.multiple_of(section * 128, 128), 128), :]
     image_unit, image_len = unit_rows(own_half)
     ihalf[0] = unit_backward(image_unit, image_len, total).astype(BF16)
@@ -417,8 +546,8 @@
 
     def wg_sum(buf, landed, ss, rs, out):
         def step(k, acc):
-            copy_to(buf.at[0], landed.at[plane(k)], ss.at[k], rs.at[plane(k)], {"dp": dp}).wait_recv()
-            return acc + landed[plane(k)].astype(F32)
+            copy_to(buf.at[0], landed.at[away(k)], ss.at[k], rs.at[away(k)], {"dp": dp}).wait_recv()
+            return acc + landed[away(k)].astype(F32)
 
         out[0] = lax.fori_loop(1, 16, step, buf[dp].astype(F32))
 
@@ -428,18 +557,24 @@
     wg_sum(wg2, wg2_in, w2_ss, w2_rs, second_out)
     wg_sum(wg1, wg1_in, w1_ss, w1_rs, first_out)
 
-    loop(16, lambda k: cols_copy(k).wait_send(), 1)
+    for copy in sends:
+        copy.wait_send()
     h_copy.wait_send()
     for n in range(14):
         weight_send(n).wait_send()
     loop(16, lambda k: cst_copy(k).wait_send(), 1)
     loop(8, lambda i: rst_copy(i).wait_send(), 1)
-    loop(8, lambda i: tshare_copy((me + i) % 8).wait_send(), 1)
-    loop(16, lambda k: ishare_copy(k).wait_send(), 1)
+    loop(4, lambda i: pass_copy(i).wait_send())
+    loop(4, lambda i: tshare_copy((x + i) % 4).wait_send(), 1)
+    for swap in both:
+        for far in (1, 2, 3):
+            image_far(swap, far).wait_send()
+            image_near(swap, far).wait_send()
     ihalf_copy.wait_send()
     for layer, sems in ((1, g1_ss), (0, g0_ss)):
-        for m in range(4):
-            pl.when(me != layer * 4 + m)(lambda m=m, layer=layer, sems=sems: g_copy(layer, m, sems).wait_send())
+        for lo in (0, 1):
+            pl.when(x != layer * 2 + lo)(lambda lo=lo, layer=layer, sems=sems: g_copy(layer, lo, sems).wait_send())
+    loop(4, lambda i: g_pass(i).wait_send())
     loop(8, lambda i: in_copy(i).wait_send(), 1)
     loop(16, lambda k: wg_copy(wg2, wg2_in, w2_ss, w2_rs, k).wait_send(), 1)
     loop(16, lambda k: wg_copy(wg1, wg1_in, w1_ss, w1_rs, k).wait_send(), 1)
@@ -461,12 +596,17 @@
         pltpu.VMEM((8, 2, 8, 128), F32),
         pltpu.VMEM((8, 128), F32),
         pltpu.VMEM((2, 16, 128), F32),
+        pltpu.VMEM((2, 16, 128), F32),
         pltpu.VMEM((16, 2, 16, 128), F32),
         pltpu.VMEM((16, 128), F32),
         pltpu.VMEM((8, 128, 512), BF16),
-        pltpu.VMEM((8, 128, 512), BF16),
-        pltpu.VMEM((16, 512, 128), BF16),
-        pltpu.VMEM((16, 512, 128), BF16),
+        pltpu.VMEM((4, 128, 512), BF16),
+        pltpu.VMEM((4, 128, 512), BF16),
+        pltpu.VMEM((2, 4, 4, 256, 128), BF16),
+        pltpu.VMEM((2, 3, 4, 256, 128), BF16),
+        pltpu.VMEM((2, 4, 256, 128), BF16),
+        pltpu.VMEM((2, 3, 256, 128), BF16),
+        pltpu.VMEM((128, 512), F32),
         pltpu.VMEM((2, 128, 512), BF16),
         pltpu.VMEM((8, 512, 512), BF16),
         pltpu.VMEM((8, 512, 512), BF16),
@@ -483,15 +623,15 @@
         pltpu.VMEM((16, 32, 512), BF16),
         pltpu.VMEM((16, 32, 512), BF16),
         pltpu.VMEM((16, 32, 512), BF16),
-        dma((16,)), dma((16,)),
+        dma((32,)), dma((64,)),
         dma((14,)), dma((16,)),
         dma((2,)),
         dma((8,)), dma((8,)),
         dma((16,)), dma((16,)),
-        dma((8,)), dma((8,)),
-        dma((16,)), dma((16,)),
+        dma((4,)), dma((4,)), dma((4,)), dma((4,)),
+        dma((6,)), dma((6,)), dma((6,)), dma((6,)),
         dma((2,)),
-        dma((4,)), dma((4,)), dma((8,)),
+        dma((2,)), dma((2,)), dma((4,)), dma((8,)),
         dma((8,)), dma((8,)),
         dma((16,)), dma((16,)), dma((16,)), dma((16,)),
     ]

time: 115 us -> 92.3 us (0.80)
  Pallas kernels: 109 us -> 86.7 us
    pallas_call x1, Pallas kernels: 109 us -> 86.7 us  [body(): pl.pallas_call(kernel, out_shape=(jax.ShapeDtypeStruct((256, 512), BF16),...]
where the time goes in v2:
time: 92.3 us; the launch traced here: 92.1 us
  Pallas kernels  86.7 us (94%)
  local copies, waits for them, and re-layouts  4.08 us (4%)
  between operations  1.3 us (1%)
    pallas_call x1, Pallas kernels, body(): pl.pallas_call(kernel, out_shape=(jax.ShapeDtypeStruct((256, 512), BF16),...  86.7 us
    unnamed x10, local copies, waits for them, and re-layouts  4.08 us

profile of v2, /device:TPU:1, one launch (start us, length us, event | category | flops | bytes accessed | tf_op | source)
XLA Modules:
  0.0 92.1 jit_solution(5852225909590483343)
XLA Ops:
  1.3 86.7 %shard_map.93 = (bf16[256,512]{1,0:T(8,128)(2,1)}, bf16[1024,256]{1,0:T(8,128)(2,1)}, f32[1,32,512]{2,1,0:T(8,128)}, f32[1,32,512]{2,1,0:T(8,128)}) custom-call(f32[1]{0:T(128)S(6)} %copy.14.scale, bf16[1024,512]{1,0:T(8,128)(2,1)} %text.1, bf16[256,512]{1,0:T(8,128)(2,1)} %image.1, bf16[1,1024,512]{2,1,0:T(8,128)(2,1)} %hin.1, bf16[1,512,512]{2,1,0:T(8,128)(2,1)} %win.1, ...), custom_call_target="tpu_custom_call" | custom-call | tf_op jit(solution)/shard_map/pallas_call | solution.py:638
  88.0 0.0 copy-start
  88.0 1.7 %copy.15 = bf16[256,512]{1,0:T(8,128)(2,1)} copy(bf16[256,512]{1,0:T(8,128)(2,1)} %get-tuple-element.8) | data formatting | bytes 524288
  89.7 0.0 copy-done
  89.7 0.0 copy-start.2
  89.7 0.8 copy.16
  90.5 0.1 copy-done.2
  90.6 0.0 copy-start.1
  90.6 0.6 copy.17
  91.2 0.2 copy-done.1
  91.4 0.6 copy.18
Async XLA Ops:
  88.0 1.7 %copy-start = (bf16[1024,256]{1,0:T(8,128)(2,1)S(1)}, bf16[1024,256]{1,0:T(8,128)(2,1)}, u32[]{:S(2)}) copy-start(bf16[1024,256]{1,0:T(8,128)(2,1)} %get-tuple-element.9) | copy-start | bytes 1572868
  89.7 0.9 copy-start.2
  90.6 0.9 copy-start.1

commit v3 on v2

v3 whole, which is shorter than its diff:
```python
import functools

import jax
import jax.numpy as jnp
from jax import lax
from jax.experimental import pallas as pl
from jax.experimental.pallas import tpu as pltpu
from jax.sharding import PartitionSpec as P

MESH = pl.DeviceIdType.MESH
F32 = jnp.float32
BF16 = jnp.bfloat16
LOW = -1e30
LOG2E = 1.4426950408889634
PIECES = (
    ((0, 1, 0, 128), (0, 3, 0, 128), (1, 0, 0, 64), (3, 0, 64, 64)),
    ((1, 0, 0, 128), (3, 0, 0, 128), (0, 1, 0, 64), (0, 3, 64, 64)),
)
ORDER = (
    (0, 0), (0, 1), (0, 3), (1, 0), (3, 0), (1, 1), (1, 3), (3, 1),
    (3, 3), (0, 2), (2, 0), (1, 2), (3, 2), (2, 1), (2, 3), (2, 2),
)


def dot_nt(a, b):
    return lax.dot_general(a, b, (((1,), (1,)), ((), ())), preferred_element_type=F32)


def dot_nn(a, b):
    return lax.dot_general(a, b, (((1,), (0,)), ((), ())), preferred_element_type=F32)


def dot_tn(a, b):
    return lax.dot_general(a, b, (((0,), (0,)), ((), ())), preferred_element_type=F32)


def unit_rows(values):
    wide = values.astype(F32)
    length = jnp.sqrt(jnp.sum(wide * wide, axis=1, keepdims=True) + 1.0)
    return wide / length, length


def unit_backward(unit, length, grad):
    return (grad - unit * jnp.sum(unit * grad, axis=1, keepdims=True)) / length


def slope_of(pre):
    s = jax.nn.sigmoid(1.702 * pre)
    return s + 1.702 * pre * s * (1.0 - s)


def rows(start, size=128):
    return pl.ds(pl.multiple_of(start, 128), size)


def copy_to(src, dst, send, recv, device):
    return pltpu.make_async_remote_copy(
        src_ref=src, dst_ref=dst, send_sem=send, recv_sem=recv, device_id=device, device_id_type=MESH
    )


def loop(count, fn, start=0):
    def step(i, _):
        fn(i)
        return 0

    lax.fori_loop(start, count, step, 0)


def kernel(
    scale, text_hbm, image_hbm, hin_hbm, win_hbm, wout_hbm,
    image_out, input_out, first_out, second_out,
    text, image, hin,
    cols, tlow, tlow_t, scores, grads, row_m, row_s, row_a,
    rst, rst_in, rst_a, own_stat, cst, cst_in, col_b,
    tshare, tpass, tshare_in, ishare, relay_in, joined, ifar_in, isum, inear_in, ifull, ihalf,
    wi_all, wo_all, hother, act, slope, slope_own, hin_t, gbuf, gin, gown, inbuf,
    wg, wfar_in, wsum, wnear_in,
    load_s, cols_ss, cols_rs, wx_ss, wx_rs, wy_ss, wy_rs, wd_ss, wd_rs, h_s, rst_ss, rst_rs, cst_ss, cst_rs,
    tp_ss, tp_rs, ts_ss, ts_rs, if_ss, if_rs, ir_ss, ir_rs, ih_s,
    g1_ss, g0_ss, gp_ss, g_rs, in_ss, in_rs,
    wf_ss, wf_rs, wn_ss, wn_rs,
):
    section = lax.axis_index("section")
    dp = lax.axis_index("dp")
    mp = lax.axis_index("mp")
    me = section * 4 + mp
    x, core = me // 2, me % 2
    z, y = dp // 4, dp % 4
    mult = scale[0]
    mult2 = mult * LOG2E

    def line(q):
        return {"section": q // 4, "mp": q % 4}

    def plane(dz, dy):
        return ((z + dz) % 4) * 4 + (y + dy) % 4

    def slot(dz, dy):
        return ORDER.index((dz % 4, dy % 4))

    def away(k):
        return plane(k // 4, k % 4)

    sends = []

    loads = [
        pltpu.make_async_copy(src, dst, load_s.at[n])
        for n, (src, dst) in enumerate(
            (
                (image_hbm.at[rows(section * 128)], image),
                (text_hbm, text),
                (win_hbm.at[0], wi_all.at[0, core]),
                (wout_hbm.at[0], wo_all.at[0, core]),
                (hin_hbm.at[0], hin),
            )
        )
    ]
    for load in loads:
        load.start()

    barrier = pltpu.get_barrier_semaphore()

    def greet_plane(k):
        pl.semaphore_signal(barrier, inc=1, device_id={"dp": away(k)}, device_id_type=MESH)

    def greet_line(i):
        pl.semaphore_signal(barrier, inc=1, device_id=line((me + i) % 8), device_id_type=MESH)

    loop(16, greet_plane, 1)
    loop(8, greet_line, 1)

    loads[0].wait()
    image_unit, image_len = unit_rows(image[...])
    cols[0] = image_unit.astype(BF16)

    def text_block(r):
        unit, _ = unit_rows(text[rows(r * 128), :])
        low = unit.astype(BF16)
        tlow[rows(r * 128), :] = low
        tlow_t[:, rows(r * 128)] = low.astype(F32).T.astype(BF16)
        row_m[rows(r * 128), :] = jnp.full((128, 128), LOW, F32)
        row_s[rows(r * 128), :] = jnp.zeros((128, 128), F32)

    pl.semaphore_wait(barrier, 22)

    def ag_send(dz, dy, lo, size, ez, ey):
        there = slot(dz - ez, dy - ey)
        copy = copy_to(
            cols.at[slot(dz, dy), lo : lo + size],
            cols.at[there, lo : lo + size],
            cols_ss.at[len(sends)],
            cols_rs.at[there * 4 + lo // 32],
            {"dp": plane(ez, ey)},
        )
        copy.start()
        sends.append(copy)

    def ag_wait(dz, dy, lo, size):
        here = slot(dz, dy)
        block = cols.at[here, lo : lo + size]
        copy_to(block, block, cols_ss.at[0], cols_rs.at[here * 4 + lo // 32], {"dp": dp}).wait_recv()

    def flip(swap, *pair):
        return pair[::-1] if swap else pair

    def half_send(swap, first, second, to_first, to_second, lo=0, size=64):
        dz, dy = flip(swap, first, second)
        ez, ey = flip(swap, to_first, to_second)
        ag_send(dz, dy, lo + 64 * swap, size, ez, ey)

    def half_wait(swap, first, second, lo=0, size=64):
        dz, dy = flip(swap, first, second)
        ag_wait(dz, dy, lo + 64 * swap, size)

    for to in ((0, 1), (0, 3), (1, 0), (3, 0)):
        for swap in (0, 1):
            half_send(swap, 0, 0, *to)

    right, left, opposite = (x + 1) % 4, (x + 3) % 4, (x + 2) % 4
    weights = (wi_all, wo_all)

    def weight_rows(which, dz=0, dy=0, lo=0, size=128):
        color = (y + dy + 2 * (z + dz)) % 4 if which == 0 else (2 * (y + dy) + z + dz) % 4
        return pl.ds(pl.multiple_of(color * 128 + lo, 64), size)

    def wx(n, which, src, dst, chip):
        at = weight_rows(which)
        ref = weights[which]
        return copy_to(
            ref.at[src, core, at], ref.at[dst, core, at], wx_ss.at[n], wx_rs.at[which * 4 + dst], line(chip * 2 + core)
        )

    wx_plan = ((0, 0, 3, right), (1, 0, 1, left), (1, 0, 3, right), (0, 0, 1, left), (0, 3, 2, right), (1, 1, 2, left))

    def wx_wait(which, rel):
        block = weights[which].at[rel, core, weight_rows(which)]
        copy_to(block, block, wx_ss.at[0], wx_rs.at[which * 4 + rel], line(me)).wait_recv()

    def wy(which, j):
        dz, dy, lo, size = PIECES[which][j]
        block = weights[which].at[pl.ds(1, 3), core, weight_rows(which, 0, 0, lo, size)]
        n = which * 4 + j
        return copy_to(block, block, wy_ss.at[n], wy_rs.at[n], {"dp": plane(4 - dz, 4 - dy)})

    def wy_wait(which, j):
        block = weights[which].at[pl.ds(1, 3), core, weight_rows(which, *PIECES[which][j])]
        n = which * 4 + j
        copy_to(block, block, wy_ss.at[n], wy_rs.at[n], {"dp": dp}).wait_recv()

    def wd(which, j, side):
        if j < 0:
            block = weights[which].at[0, side]
        else:
            at = weight_rows(which) if j == 4 else weight_rows(which, *PIECES[which][j])
            block = weights[which].at[pl.ds(1, 3), side, at]
        n = which * 6 + j + 1
        return copy_to(block, block, wd_ss.at[n], wd_rs.at[n], line(x * 2 + 1 - core))

    twin = (1 - section) * 4 + mp
    h_copy = copy_to(hin.at[rows(twin * 128), :], hother, h_s.at[0], h_s.at[1], line(twin))
    for load in loads[2:]:
        load.wait()
    for n in range(4):
        wx(n, *wx_plan[n]).start()
    for which in (0, 1):
        wd(which, -1, core).start()
    h_copy.start()

    def score_pair(p):
        pair = cols[pl.ds(2 * p, 2)].reshape(256, 512)
        part = dot_nt(tlow[...], pair)
        c_m, c_s = jnp.full((8, 256), LOW, F32), jnp.zeros((8, 256), F32)
        for r in range(8):
            at = slice(r * 128, (r + 1) * 128)
            s = part[at] * mult2
            scores[p, at, :] = s
            s3 = s.reshape(16, 8, 256)
            n_m = jnp.maximum(c_m, jnp.max(s3, axis=0))
            c_s = c_s * jnp.exp2(c_m - n_m) + jnp.sum(jnp.exp2(s3 - n_m[None]), axis=0)
            c_m = n_m
            old = row_m[at, :]
            s0, s1 = s[:, :128], s[:, 128:]
            new = jnp.maximum(old, jnp.maximum(s0, s1))
            row_s[at, :] = row_s[at, :] * jnp.exp2(old - new) + jnp.exp2(s0 - new) + jnp.exp2(s1 - new)
            row_m[at, :] = new

        peak = jnp.max(c_m, axis=0, keepdims=True)
        total = peak + jnp.log2(jnp.sum(c_s * jnp.exp2(c_m - peak), axis=0, keepdims=True))
        for j in (0, 1):
            own_stat[pl.ds(2 * p + j, 1), :] = total[:, j * 128 : (j + 1) * 128]

    def spread(swap, first, second):
        for to in (1, 3):
            half_send(swap, first, second, to, 0)

    both = (0, 1)
    loads[1].wait()
    loop(8, text_block)
    for swap in both:
        half_wait(swap, 0, 1)
        half_wait(swap, 0, 3)
        half_send(swap, 0, 1, 0, 3, 0, 32)
        half_send(swap, 0, 3, 0, 1, 32, 32)
    for swap in both:
        spread(swap, 0, 1)
        spread(swap, 0, 3)
    for swap in both:
        half_wait(swap, 1, 0)
        half_send(swap, 1, 0, 3, 0)
        half_wait(swap, 3, 0)
    loop(2, score_pair)
    for swap in both:
        half_wait(swap, 0, 2, 0, 32)
        half_wait(swap, 0, 2, 32, 32)
        spread(swap, 0, 2)
    for swap in both:
        for second in (1, 3):
            half_wait(swap, 3, second)
            half_send(swap, 3, second, 1, 0)
            half_wait(swap, 1, second)
    wx_wait(0, 3)
    wx(4, *wx_plan[4]).start()
    wx_wait(1, 1)
    wx(5, *wx_plan[5]).start()
    loop(4, score_pair, 2)
    for swap in both:
        half_wait(swap, 1, 2)
        half_send(swap, 1, 2, 3, 0)
        half_wait(swap, 3, 2)
    for swap in both:
        half_wait(swap, 2, 0)
    half_wait(1, 2, 1)
    loop(6, score_pair, 4)
    half_wait(0, 2, 1)
    for swap in both:
        half_wait(swap, 2, 3)
    for which in both:
        wx_wait(which, 1 if which == 0 else 3)
        wx_wait(which, 2)
    for j in (2, 3):
        for which in both:
            wy(which, j).start()
    for which in both:
        wd(which, 4, core).start()
    loop(7, score_pair, 6)
    for swap in both:
        half_wait(swap, 2, 2)
    score_pair(7)
    for k, (dz, dy) in enumerate(ORDER):
        cst[pl.ds(plane(dz, dy), 1), :] = own_stat[k : k + 1, :]

    def cst_copy(k):
        dz, dy = ORDER[k]
        return copy_to(cst, cst_in.at[dp], cst_ss.at[k], cst_rs.at[dp], {"dp": plane(dz, dy)})

    def cst_wait(k):
        copy_to(cst, cst_in.at[away(k)], cst_ss.at[k], cst_rs.at[away(k)], {"dp": dp}).wait_recv()

    for k in range(15, 0, -1):
        cst_copy(k).start()
    for j in both:
        for which in both:
            wy(which, j).start()
    cst_in[dp] = cst[...]

    for r in range(8):
        m_t = row_m[r * 128 : (r + 1) * 128, :].T
        s_t = row_s[r * 128 : (r + 1) * 128, :].T
        peak = jnp.max(m_t, axis=0, keepdims=True)
        rst[r : r + 1, :] = peak + jnp.log2(jnp.sum(s_t * jnp.exp2(m_t - peak), axis=0, keepdims=True))

    def rst_copy(i):
        q = (me + i) % 8
        return copy_to(rst, rst_in.at[me], rst_ss.at[i], rst_rs.at[me], line(q))

    def rst_wait(i):
        q = (me + i) % 8
        copy_to(rst, rst_in.at[q], rst_ss.at[i], rst_rs.at[q], line(me)).wait_recv()

    loop(8, lambda i: rst_copy(i).start(), 1)
    rst_in[me] = rst[...]

    def hidden_block(r):
        at = rows(r * 128)
        h = hin[at, :]
        pre = dot_nn(h, wi_all[0, core])
        sig = jax.nn.sigmoid(1.702 * pre)
        act[at, :] = (pre * sig).astype(BF16)
        slope[at, :] = sig + 1.702 * pre * sig * (1.0 - sig)
        hin_t[:, at] = h.astype(F32).T.astype(BF16)

    loop(8, hidden_block)

    loop(8, rst_wait, 1)
    peak = jnp.max(rst_in[...], axis=0)
    total = jnp.sum(jnp.exp2(rst_in[...] - peak[None]), axis=0)
    rst_a[...] = peak + jnp.log2(2.0 * total)
    for r in range(8):
        row_a[r * 128 : (r + 1) * 128, :] = jnp.broadcast_to(rst_a[r : r + 1, :], (128, 128)).T

    loop(16, cst_wait, 1)
    peak = jnp.max(cst_in[...], axis=0)
    total = jnp.sum(jnp.exp2(cst_in[...] - peak[None]), axis=0)
    own_stat[...] = peak + jnp.log2(2.0 * total)
    for k, (dz, dy) in enumerate(ORDER):
        col_b[k : k + 1, :] = own_stat[pl.ds(plane(dz, dy), 1), :]

    def prob(s, at, b):
        return jnp.exp2(s - row_a[at, :]) + jnp.exp2(s - b)

    def pass_copy(chip):
        other = chip * 2 + 1 - core
        return copy_to(tshare.at[other], tpass.at[chip], tp_ss.at[chip], tp_rs.at[chip], line(x * 2 + 1 - core))

    def tshare_copy(chip):
        own = chip * 2 + core
        return copy_to(tshare.at[own], tshare_in.at[x], ts_ss.at[chip], ts_rs.at[x], line(own))

    def text_part(chip):
        def grad_block(t):
            p = t % 8
            at = rows(chip * 256 + (t // 8) * 128)
            for j in (0, 1):
                s = scores[p, at, j * 128 : (j + 1) * 128]
                b = col_b[pl.ds(2 * p + j, 1), :]
                grads[at, pl.ds(pl.multiple_of(p * 256 + j * 128, 128), 128)] = prob(s, at, b).astype(BF16)

        loop(16, grad_block)

        mine = 2 * mp + section

        @pl.when(mine // 2 == chip)
        def _():
            at = rows(mine * 128)
            s = scores[0, at, :128]
            eye = lax.broadcasted_iota(jnp.int32, (128, 128), 0) == lax.broadcasted_iota(jnp.int32, (128, 128), 1)
            part = prob(s, at, col_b[0:1, :])
            grads[at, :128] = (part - jnp.where(eye, 1.0, 0.0)).astype(BF16)

        part = dot_nn(grads[rows(chip * 256, 256), :], cols[...].reshape(2048, 512))
        for j in (0, 1):
            tshare[chip * 2 + j] = part[j * 128 : (j + 1) * 128].astype(BF16)
        pass_copy(chip).start()

    def text_merge(chip):
        own = chip * 2 + core
        pass_copy(chip).wait_recv()
        tshare[own] = (tshare[own].astype(F32) + tpass[chip].astype(F32)).astype(BF16)

    def text_step(i):
        chip = jnp.where(i == 0, opposite, jnp.where(i == 1, right, jnp.where(i == 2, left, x)))
        last = jnp.where(i == 1, opposite, jnp.where(i == 2, right, left))
        text_part(chip)

        @pl.when(i > 0)
        def _():
            text_merge(last)
            tshare_copy(last).start()

    def wd_pass(pieces):
        for j in pieces:
            for which in both:
                wy_wait(which, j)
                wd(which, j, core).start()

    wd_pass((2, 3))
    loop(4, text_step)
    text_merge(x)
    wd_pass((0, 1))

    def image_part(p):
        part = dot_nn(tlow_t[...], grads[:, p * 256 : (p + 1) * 256])
        for j in (0, 1):
            dz, dy = ORDER[2 * p + j]
            block = part[:, j * 128 : (j + 1) * 128].astype(BF16)
            ishare[0, dz, dy] = block[:256]
            ishare[1, dy, dz] = block[256:]

    def step_of(swap, far):
        return {"dp": plane(*flip(swap, far, 0))}

    def image_far(n, swap):
        src, dst, to = (
            (ishare.at[swap, 2, 0:2], relay_in.at[swap, 0], 1),
            (ishare.at[swap, 2, 2:4], relay_in.at[swap, 1], 3),
            (ishare.at[swap, 1, 2:4], ifar_in.at[swap, 0, 2:4], 1),
            (ishare.at[swap, 3, 0:2], ifar_in.at[swap, 1, 0:2], 3),
            (joined.at[swap, 0], ifar_in.at[swap, 0, 0:2], 1),
            (joined.at[swap, 1], ifar_in.at[swap, 1, 2:4], 3),
        )[n]
        k = swap * 6 + n
        return copy_to(src, dst, if_ss.at[k], if_rs.at[k], step_of(swap, to))

    def image_near(swap, far):
        n = swap * 3 + 3 - far
        return copy_to(isum.at[swap, far], inear_in.at[swap, 3 - far], ir_ss.at[n], ir_rs.at[n], step_of(1 - swap, far))

    for p in range(7, -1, -1):
        image_part(p)
    for n in range(4):
        for swap in both:
            image_far(n, swap).start()

    def image_relay():
        for n, far, lo in ((0, 1, 0), (1, 3, 2)):
            for swap in both:
                image_far(n, swap).wait_recv()
                joined[swap, n] = (
                    ishare[swap, far, lo : lo + 2].astype(F32) + relay_in[swap, n].astype(F32)
                ).astype(BF16)
                image_far(n + 4, swap).start()


    h_copy.wait_recv()

    for j in range(-1, 5):
        for which in both:
            wd(which, j, 1 - core).wait_recv()

    def home(q):
        return (q // 2 + 4 - x) % 4, q % 2

    def own_block(r):
        h = jnp.where(r // 4 == section, hin[rows(me * 128), :], hother[...])
        slope_own[r] = slope_of(dot_nn(h, wi_all[home(r)]))

    loop(8, own_block)

    def tshare_sum(i, acc):
        chip = (x + i) % 4
        copy_to(tshare.at[0], tshare_in.at[chip], ts_ss.at[chip], ts_rs.at[chip], line(me)).wait_recv()
        return acc + tshare_in[chip].astype(F32)

    total = lax.fori_loop(1, 4, tshare_sum, tshare[me].astype(F32)) * mult
    unit, length = unit_rows(text[rows(me * 128), :])
    gown[0] = unit_backward(unit, length, total).astype(BF16)

    def g_copy(layer, lo, sems):
        to = {"section": layer, "mp": lo * 2 + core}
        return copy_to(gown.at[1 - layer], gbuf.at[me], sems.at[lo], g_rs.at[me], to)

    def g_send(layer, sems):
        for lo in (0, 1):
            pl.when(x != layer * 2 + lo)(lambda lo=lo: g_copy(layer, lo, sems).start())

        @pl.when(section == layer)
        def _():
            gbuf[me] = gown[1 - layer]

    def g_pass(i):
        q = ((x + i) % 4) * 2 + core
        return copy_to(gbuf.at[q], gbuf.at[q], gp_ss.at[i], g_rs.at[q], line(x * 2 + 1 - core))

    def g_arrive(q):
        copy_to(gbuf.at[q], gbuf.at[q], gp_ss.at[0], g_rs.at[q], line(me)).wait_recv()

    def g_relay(i):
        g_arrive(((x + i) % 4) * 2 + core)
        g_pass(i).start()

    def chain(layer):
        g = gown[1 - layer]

        def step(j, acc):
            q = layer * 4 + j
            back = dot_nt(g, wo_all[home(q)])
            pre_grad = (back * slope_own[q]).astype(BF16)
            return acc + dot_nt(pre_grad, wi_all[home(q)])

        return lax.fori_loop(0, 4, step, g.astype(F32)).astype(BF16)

    g_send(1, g1_ss)
    gown[1] = chain(1)
    g_send(0, g0_ss)
    image_relay()
    lowest = chain(0)
    gin[0] = lowest[:, :256]
    gin[1] = lowest[:, 256:]

    def in_copy(i):
        q = (me + i) % 8
        return copy_to(gin.at[q // 4], inbuf.at[me], in_ss.at[i], in_rs.at[me], line(q))

    def image_fold(swap):
        for n in range(2, 6):
            image_far(n, swap).wait_recv()
        total = ishare[swap, 0].astype(F32) + ifar_in[swap, 0].astype(F32) + ifar_in[swap, 1].astype(F32)
        isum[swap] = total.astype(BF16)
        for far in (2, 1, 3):
            image_near(swap, far).start()

    g_pass(0).start()
    loop(4, g_relay, 1)
    loop(8, lambda i: in_copy(i).start(), 1)
    inbuf[me] = gin[section]
    for swap in both:
        image_fold(swap)
    loop(4, lambda i: g_arrive(((x + i) % 4) * 2 + 1 - core))

    full = gbuf[...].reshape(1024, 512)

    def put_weight(which, value):
        for zz in range(4):
            for yy in range(4):
                block = value[(zz * 4 + yy) * 32 : (zz * 4 + yy + 1) * 32].astype(BF16)
                wg[which, 0, zz, yy] = block[:, :256]
                wg[which, 1, yy, zz] = block[:, 256:]

    def weight_far(which, swap, far):
        n = which * 6 + swap * 3 + 3 - far
        at = ((y if swap else z) + far) % 4
        return copy_to(
            wg.at[which, swap, at], wfar_in.at[which, swap, 3 - far], wf_ss.at[n], wf_rs.at[n], step_of(swap, far)
        )

    def weight_near(which, swap, far):
        n = which * 6 + swap * 3 + 3 - far
        at = ((z if swap else y) + far) % 4
        return copy_to(
            wsum.at[which, swap, at], wnear_in.at[which, swap, 3 - far], wn_ss.at[n], wn_rs.at[n], step_of(1 - swap, far)
        )

    def send_all(step, which):
        for far in (2, 1, 3):
            for swap in both:
                step(which, swap, far).start()

    def weight_fold(which):
        for swap in both:
            total = wg[which, swap, y if swap else z].astype(F32)
            for far in (1, 2, 3):
                landed = wfar_in.at[which, swap, far - 1]
                n = which * 6 + swap * 3 + far - 1
                copy_to(landed, landed, wf_ss.at[n], wf_rs.at[n], {"dp": dp}).wait_recv()
                total = total + landed[...].astype(F32)
            wsum[which, swap] = total.astype(BF16)
        send_all(weight_near, which)

    def weight_end(which, out):
        for swap in both:
            total = wsum[which, swap, z if swap else y].astype(F32)
            for far in (1, 2, 3):
                landed = wnear_in.at[which, swap, far - 1]
                n = which * 6 + swap * 3 + far - 1
                copy_to(landed, landed, wn_ss.at[n], wn_rs.at[n], {"dp": dp}).wait_recv()
                total = total + landed[...].astype(F32)
            out[0, :, swap * 256 : (swap + 1) * 256] = total

    put_weight(1, dot_tn(full, act[...]))
    send_all(weight_far, 1)

    def back_block(r):
        at = rows(r * 256, 256)
        back = dot_nt(gbuf[pl.ds(2 * r, 2)].reshape(256, 512), wo_all[0, core])
        act[at, :] = (back * slope[at, :]).astype(BF16)

    loop(4, back_block)
    put_weight(0, dot_nn(hin_t[...], act[...]))
    send_all(weight_far, 0)

    for swap in both:
        total = isum[swap, 0].astype(F32)
        for far in (1, 2, 3):
            landed = inear_in.at[swap, far - 1]
            copy_to(landed, landed, ir_ss.at[0], ir_rs.at[swap * 3 + far - 1], {"dp": dp}).wait_recv()
            total = total + landed[...].astype(F32)
        ifull[:, swap * 256 : (swap + 1) * 256] = total.T
    total = ifull[...] * mult
    image_unit, image_len = unit_rows(image[...])
    ihalf[0] = unit_backward(image_unit, image_len, total).astype(BF16)
    ihalf_copy = copy_to(ihalf.at[0], ihalf.at[1], ih_s.at[0], ih_s.at[1], line(twin))
    ihalf_copy.start()
    weight_fold(1)

    def in_wait(i):
        q = (me + i) % 8
        copy_to(gin.at[0], inbuf.at[q], in_ss.at[i], in_rs.at[q], line(me)).wait_recv()

    loop(8, in_wait, 1)
    input_out[...] = inbuf[...].reshape(1024, 256)

    weight_fold(0)
    image_out[rows(section * 128), :] = ihalf[0]
    ihalf_copy.wait_recv()
    image_out[rows((1 - section) * 128), :] = ihalf[1]
    weight_end(1, second_out)
    weight_end(0, first_out)
    for copy in sends:
        copy.wait_send()
    h_copy.wait_send()
    for n in range(6):
        wx(n, *wx_plan[n]).wait_send()
    for which in both:
        for j in range(4):
            wy(which, j).wait_send()
        for j in range(-1, 5):
            wd(which, j, core).wait_send()
    for k in range(1, 16):
        cst_copy(k).wait_send()
    loop(8, lambda i: rst_copy(i).wait_send(), 1)
    loop(4, lambda i: pass_copy(i).wait_send())
    loop(4, lambda i: tshare_copy((x + i) % 4).wait_send(), 1)
    for swap in both:
        for far in (1, 2, 3):
            image_near(swap, far).wait_send()
        for n in range(6):
            image_far(n, swap).wait_send()
    ihalf_copy.wait_send()
    for layer, sems in ((1, g1_ss), (0, g0_ss)):
        for lo in (0, 1):
            pl.when(x != layer * 2 + lo)(lambda lo=lo, layer=layer, sems=sems: g_copy(layer, lo, sems).wait_send())
    loop(4, lambda i: g_pass(i).wait_send())
    loop(8, lambda i: in_copy(i).wait_send(), 1)
    for which in both:
        for swap in both:
            for far in (1, 2, 3):
                weight_far(which, swap, far).wait_send()
                weight_near(which, swap, far).wait_send()


def settle(*refs):
    for src, dst in zip(refs[:4], refs[4:]):
        dst[...] = src[...]


def body(text_feats, image_feats, logit_scale, layer_inputs, w_in, w_out):
    vmem = pl.BlockSpec(memory_space=pltpu.VMEM)
    dma = pltpu.SemaphoreType.DMA
    scratch = [
        pltpu.VMEM((1024, 512), BF16),
        pltpu.VMEM((128, 512), BF16),
        pltpu.VMEM((1024, 512), BF16),
        pltpu.VMEM((16, 128, 512), BF16),
        pltpu.VMEM((1024, 512), BF16),
        pltpu.VMEM((512, 1024), BF16),
        pltpu.VMEM((8, 1024, 256), F32),
        pltpu.VMEM((1024, 2048), BF16),
        pltpu.VMEM((1024, 128), F32),
        pltpu.VMEM((1024, 128), F32),
        pltpu.VMEM((1024, 128), F32),
        pltpu.VMEM((8, 128), F32),
        pltpu.VMEM((8, 8, 128), F32),
        pltpu.VMEM((8, 128), F32),
        pltpu.VMEM((16, 128), F32),
        pltpu.VMEM((16, 128), F32),
        pltpu.VMEM((16, 16, 128), F32),
        pltpu.VMEM((16, 128), F32),
        pltpu.VMEM((8, 128, 512), BF16),
        pltpu.VMEM((4, 128, 512), BF16),
        pltpu.VMEM((4, 128, 512), BF16),
        pltpu.VMEM((2, 4, 4, 256, 128), BF16),
        pltpu.VMEM((2, 2, 2, 256, 128), BF16),
        pltpu.VMEM((2, 2, 2, 256, 128), BF16),
        pltpu.VMEM((2, 2, 4, 256, 128), BF16),
        pltpu.VMEM((2, 4, 256, 128), BF16),
        pltpu.VMEM((2, 3, 256, 128), BF16),
        pltpu.VMEM((128, 512), F32),
        pltpu.VMEM((2, 128, 512), BF16),
        pltpu.VMEM((4, 2, 512, 512), BF16),
        pltpu.VMEM((4, 2, 512, 512), BF16),
        pltpu.VMEM((128, 512), BF16),
        pltpu.VMEM((1024, 512), BF16),
        pltpu.VMEM((1024, 512), F32),
        pltpu.VMEM((8, 128, 512), F32),
        pltpu.VMEM((512, 1024), BF16),
        pltpu.VMEM((8, 128, 512), BF16),
        pltpu.VMEM((2, 128, 256), BF16),
        pltpu.VMEM((2, 128, 512), BF16),
        pltpu.VMEM((8, 128, 256), BF16),
        pltpu.VMEM((2, 2, 4, 4, 32, 256), BF16),
        pltpu.VMEM((2, 2, 3, 4, 32, 256), BF16),
        pltpu.VMEM((2, 2, 4, 32, 256), BF16),
        pltpu.VMEM((2, 2, 3, 32, 256), BF16),
        dma((5,)),
        dma((32,)), dma((64,)),
        dma((6,)), dma((8,)), dma((8,)), dma((8,)), dma((12,)), dma((12,)),
        dma((2,)),
        dma((8,)), dma((8,)),
        dma((16,)), dma((16,)),
        dma((4,)), dma((4,)), dma((4,)), dma((4,)),
        dma((12,)), dma((12,)), dma((6,)), dma((6,)),
        dma((2,)),
        dma((2,)), dma((2,)), dma((4,)), dma((8,)),
        dma((8,)), dma((8,)),
        dma((12,)), dma((12,)), dma((12,)), dma((12,)),
    ]
    results = pl.pallas_call(
        kernel,
        out_shape=(
            jax.ShapeDtypeStruct((256, 512), BF16),
            jax.ShapeDtypeStruct((1024, 256), BF16),
            jax.ShapeDtypeStruct((1, 32, 512), F32),
            jax.ShapeDtypeStruct((1, 32, 512), F32),
        ),
        in_specs=[pl.BlockSpec(memory_space=pltpu.SMEM)] + [pl.BlockSpec(memory_space=pl.ANY)] * 5,
        out_specs=(vmem,) * 4,
        scratch_shapes=scratch,
        compiler_params=pltpu.CompilerParams(
            collective_id=0, has_side_effects=True, vmem_limit_bytes=56 * 1024 * 1024
        ),
    )(logit_scale, text_feats, image_feats, layer_inputs, w_in, w_out)
    return pl.pallas_call(
        settle,
        out_shape=tuple(jax.ShapeDtypeStruct(r.shape, r.dtype) for r in results),
        in_specs=[vmem] * 4,
        out_specs=(vmem,) * 4,
    )(*results)


def solution(mesh):
    placed = (
        P("dp", None),
        P(("dp", "mp"), None),
        P(),
        P("section", "dp", None),
        P("section", None, "mp"),
        P("section", "mp", None),
    )
    return jax.shard_map(
        body,
        mesh=mesh,
        in_specs=placed,
        out_specs=(
            P(("dp", "mp"), None),
            P("dp", "section"),
            P("section", "dp", "mp"),
            P("section", "dp", "mp"),
        ),
        check_vma=False,
    )
```

time: 92.3 us -> 79.5 us (0.86)
  Pallas kernels: 86.7 us -> 77.3 us
  local copies, waits for them, and re-layouts: 4.08 us -> 0 us
    pallas_call x1, Pallas kernels: 86.7 us -> 75.3 us  [body(): pl.pallas_call(kernel, out_shape=(jax.ShapeDtypeStruct((256, 512), BF16),...]
    unnamed x10 -> x0, local copies, waits for them, and re-layouts: 4.08 us -> none
    pallas_call x0 -> x1, Pallas kernels: none -> 2.06 us  [body(): pl.pallas_call(settle, out_shape=tuple((jax.ShapeDtypeStruct(r.shape, r.d...]
where the time goes in v3:
time: 79.5 us; the launch traced here: 78.6 us
  Pallas kernels  77.3 us (97%)
  between operations  1.29 us (2%)
    pallas_call x1, Pallas kernels, body(): pl.pallas_call(kernel, out_shape=(jax.ShapeDtypeStruct((256, 512), BF16),...  75.3 us
    pallas_call x1, Pallas kernels, body(): pl.pallas_call(settle, out_shape=tuple((jax.ShapeDtypeStruct(r.shape, r.d...  2.06 us

profile of v3, /device:TPU:1, one launch (start us, length us, event | category | flops | bytes accessed | tf_op | source)
XLA Modules:
  0.0 78.6 jit_solution(2062193928812464028)
XLA Ops:
  1.3 75.3 %shard_map.93 = (bf16[256,512]{1,0:T(8,128)(2,1)}, bf16[1024,256]{1,0:T(8,128)(2,1)}, f32[1,32,512]{2,1,0:T(8,128)}, f32[1,32,512]{2,1,0:T(8,128)}) custom-call(f32[1]{0:T(128)S(6)} %copy.10.scale, bf16[1024,512]{1,0:T(8,128)(2,1)} %text_hbm.1, bf16[256,512]{1,0:T(8,128)(2,1)} %image_hbm.1, bf16[1,1024,512]{2,1,0:T(8,128)(2,1)} %hin_hbm.1, ...), custom_call_target="tpu_custom_call" | custom-call | tf_op jit(solution)/shard_map/pallas_call | solution.py:748
  76.5 2.1 %shard_map.94 = (bf16[256,512]{1,0:T(8,128)(2,1)}, bf16[1024,256]{1,0:T(8,128)(2,1)}, f32[1,32,512]{2,1,0:T(8,128)}, f32[1,32,512]{2,1,0:T(8,128)}) custom-call(bf16[256,512]{1,0:T(8,128)(2,1)} %get-tuple-element.8.refs_0_, bf16[1024,256]{1,0:T(8,128)(2,1)} %get-tuple-element.9.refs_1_, f32[1,32,512]{2,1,0:T(8,128)} %get-tuple-element.10.refs_2_, ...), custom_call_target="tpu_custom_call" | custom-call | tf_op jit(solution)/shard_map/pallas_call | solution.py:763

commit v4 on v3

--- a/solution.py
+++ b/solution.py
@@ -12,10 +12,7 @@
 BF16 = jnp.bfloat16
 LOW = -1e30
 LOG2E = 1.4426950408889634
-PIECES = (
-    ((0, 1, 0, 128), (0, 3, 0, 128), (1, 0, 0, 64), (3, 0, 64, 64)),
-    ((1, 0, 0, 128), (3, 0, 0, 128), (0, 1, 0, 64), (0, 3, 64, 64)),
-)
+AROUND = ((0, 1), (0, 3), (1, 0), (3, 0))
 ORDER = (
     (0, 0), (0, 1), (0, 3), (1, 0), (3, 0), (1, 1), (1, 3), (3, 1),
     (3, 3), (0, 2), (2, 0), (1, 2), (3, 2), (2, 1), (2, 3), (2, 2),
@@ -71,14 +68,14 @@
     scale, text_hbm, image_hbm, hin_hbm, win_hbm, wout_hbm,
     image_out, input_out, first_out, second_out,
     text, image, hin,
-    cols, tlow, tlow_t, scores, grads, row_m, row_s, row_a,
+    cols, tlow, tlow_t, scores, grads0, grads1, grads2, grads3, row_m, row_s, row_a,
     rst, rst_in, rst_a, own_stat, cst, cst_in, col_b,
     tshare, tpass, tshare_in, ishare, relay_in, joined, ifar_in, isum, inear_in, ifull, ihalf,
     wi_all, wo_all, hother, act, slope, slope_own, hin_t, gbuf, gin, gown, inbuf,
-    wg, wfar_in, wsum, wnear_in,
+    wacc, wg, wrelay_in, wjoined, wfar_in, wsum, wnear_in,
     load_s, cols_ss, cols_rs, wx_ss, wx_rs, wy_ss, wy_rs, wd_ss, wd_rs, h_s, rst_ss, rst_rs, cst_ss, cst_rs,
     tp_ss, tp_rs, ts_ss, ts_rs, if_ss, if_rs, ir_ss, ir_rs, ih_s,
-    g1_ss, g0_ss, gp_ss, g_rs, in_ss, in_rs,
+    g1_ss, g0_ss, gf_ss, g_rs, gp_ss, gp_rs, in_ss, in_rs,
     wf_ss, wf_rs, wn_ss, wn_rs,
 ):
     section = lax.axis_index("section")
@@ -180,12 +177,11 @@
     right, left, opposite = (x + 1) % 4, (x + 3) % 4, (x + 2) % 4
     weights = (wi_all, wo_all)
 
-    def weight_rows(which, dz=0, dy=0, lo=0, size=128):
-        color = (y + dy + 2 * (z + dz)) % 4 if which == 0 else (2 * (y + dy) + z + dz) % 4
-        return pl.ds(pl.multiple_of(color * 128 + lo, 64), size)
+    def weight_rows(turn, lo=0, size=256):
+        return pl.ds(pl.multiple_of((y + z + turn) % 2 * 256 + lo, 64), size)
 
     def wx(n, which, src, dst, chip):
-        at = weight_rows(which)
+        at = weight_rows(0)
         ref = weights[which]
         return copy_to(
             ref.at[src, core, at], ref.at[dst, core, at], wx_ss.at[n], wx_rs.at[which * 4 + dst], line(chip * 2 + core)
@@ -194,17 +190,17 @@
     wx_plan = ((0, 0, 3, right), (1, 0, 1, left), (1, 0, 3, right), (0, 0, 1, left), (0, 3, 2, right), (1, 1, 2, left))
 
     def wx_wait(which, rel):
-        block = weights[which].at[rel, core, weight_rows(which)]
+        block = weights[which].at[rel, core, weight_rows(0)]
         copy_to(block, block, wx_ss.at[0], wx_rs.at[which * 4 + rel], line(me)).wait_recv()
 
     def wy(which, j):
-        dz, dy, lo, size = PIECES[which][j]
-        block = weights[which].at[pl.ds(1, 3), core, weight_rows(which, 0, 0, lo, size)]
+        dz, dy = AROUND[j]
+        block = weights[which].at[pl.ds(1, 3), core, weight_rows(0, j * 64, 64)]
         n = which * 4 + j
         return copy_to(block, block, wy_ss.at[n], wy_rs.at[n], {"dp": plane(4 - dz, 4 - dy)})
 
     def wy_wait(which, j):
-        block = weights[which].at[pl.ds(1, 3), core, weight_rows(which, *PIECES[which][j])]
+        block = weights[which].at[pl.ds(1, 3), core, weight_rows(1, j * 64, 64)]
         n = which * 4 + j
         copy_to(block, block, wy_ss.at[n], wy_rs.at[n], {"dp": dp}).wait_recv()
 
@@ -212,7 +208,7 @@
         if j < 0:
             block = weights[which].at[0, side]
         else:
-            at = weight_rows(which) if j == 4 else weight_rows(which, *PIECES[which][j])
+            at = weight_rows(0) if j == 4 else weight_rows(1, j * 64, 64)
             block = weights[which].at[pl.ds(1, 3), side, at]
         n = which * 6 + j + 1
         return copy_to(block, block, wd_ss.at[n], wd_rs.at[n], line(x * 2 + 1 - core))
@@ -295,14 +291,6 @@
     half_wait(0, 2, 1)
     for swap in both:
         half_wait(swap, 2, 3)
-    for which in both:
-        wx_wait(which, 1 if which == 0 else 3)
-        wx_wait(which, 2)
-    for j in (2, 3):
-        for which in both:
-            wy(which, j).start()
-    for which in both:
-        wd(which, 4, core).start()
     loop(7, score_pair, 6)
     for swap in both:
         half_wait(swap, 2, 2)
@@ -319,9 +307,6 @@
 
     for k in range(15, 0, -1):
         cst_copy(k).start()
-    for j in both:
-        for which in both:
-            wy(which, j).start()
     cst_in[dp] = cst[...]
 
     for r in range(8):
@@ -366,9 +351,6 @@
     for k, (dz, dy) in enumerate(ORDER):
         col_b[k : k + 1, :] = own_stat[pl.ds(plane(dz, dy), 1), :]
 
-    def prob(s, at, b):
-        return jnp.exp2(s - row_a[at, :]) + jnp.exp2(s - b)
-
     def pass_copy(chip):
         other = chip * 2 + 1 - core
         return copy_to(tshare.at[other], tpass.at[chip], tp_ss.at[chip], tp_rs.at[chip], line(x * 2 + 1 - core))
@@ -377,60 +359,65 @@
         own = chip * 2 + core
         return copy_to(tshare.at[own], tshare_in.at[x], ts_ss.at[chip], ts_rs.at[x], line(own))
 
-    def text_part(chip):
-        def grad_block(t):
-            p = t % 8
-            at = rows(chip * 256 + (t // 8) * 128)
-            for j in (0, 1):
+    chips = (opposite, right, left, x)
+    parts = (grads0, grads1, grads2, grads3)
+    mine = 2 * mp + section
+    eye = (
+        lax.broadcasted_iota(jnp.int32, (128, 128), 0) == lax.broadcasted_iota(jnp.int32, (128, 128), 1)
+    ).astype(F32)
+
+    def make_grads(i):
+        for half in both:
+            at = rows(chips[i] * 256 + half * 128)
+            a = row_a[at, :]
+            for k in range(16):
+                p, j = k // 2, k % 2
                 s = scores[p, at, j * 128 : (j + 1) * 128]
-                b = col_b[pl.ds(2 * p + j, 1), :]
-                grads[at, pl.ds(pl.multiple_of(p * 256 + j * 128, 128), 128)] = prob(s, at, b).astype(BF16)
-
-        loop(16, grad_block)
-
-        mine = 2 * mp + section
-
-        @pl.when(mine // 2 == chip)
-        def _():
-            at = rows(mine * 128)
-            s = scores[0, at, :128]
-            eye = lax.broadcasted_iota(jnp.int32, (128, 128), 0) == lax.broadcasted_iota(jnp.int32, (128, 128), 1)
-            part = prob(s, at, col_b[0:1, :])
-            grads[at, :128] = (part - jnp.where(eye, 1.0, 0.0)).astype(BF16)
-
-        part = dot_nn(grads[rows(chip * 256, 256), :], cols[...].reshape(2048, 512))
-        for j in (0, 1):
-            tshare[chip * 2 + j] = part[j * 128 : (j + 1) * 128].astype(BF16)
-        pass_copy(chip).start()
+                part = jnp.exp2(s - a) + jnp.exp2(s - col_b[k : k + 1, :])
+                if k == 0:
+                    part = part - eye * jnp.where(chips[i] * 2 + half == mine, 1.0, 0.0)
+                parts[i][half * 128 : (half + 1) * 128, k * 128 : (k + 1) * 128] = part.astype(BF16)
 
     def text_merge(chip):
         own = chip * 2 + core
         pass_copy(chip).wait_recv()
         tshare[own] = (tshare[own].astype(F32) + tpass[chip].astype(F32)).astype(BF16)
 
-    def text_step(i):
-        chip = jnp.where(i == 0, opposite, jnp.where(i == 1, right, jnp.where(i == 2, left, x)))
-        last = jnp.where(i == 1, opposite, jnp.where(i == 2, right, left))
-        text_part(chip)
-
-        @pl.when(i > 0)
-        def _():
-            text_merge(last)
-            tshare_copy(last).start()
-
-    def wd_pass(pieces):
-        for j in pieces:
-            for which in both:
-                wy_wait(which, j)
-                wd(which, j, core).start()
-
-    wd_pass((2, 3))
-    loop(4, text_step)
+    def wd_pass(which):
+        for j in range(4):
+            wy_wait(which, j)
+            wd(which, j, core).start()
+
+    def wd_wait(which):
+        for j in range(-1, 5):
+            wd(which, j, 1 - core).wait_recv()
+
+    for which in both:
+        wx_wait(which, 1 if which == 0 else 3)
+        wx_wait(which, 2)
+    for which in both:
+        for j in range(4):
+            wy(which, j).start()
+    for which in both:
+        wd(which, 4, core).start()
+    make_grads(0)
+    for i in range(4):
+        if i < 3:
+            make_grads(i + 1)
+        part = dot_nn(parts[i][...], cols[...].reshape(2048, 512))
+        for j in (0, 1):
+            tshare[chips[i] * 2 + j] = part[j * 128 : (j + 1) * 128].astype(BF16)
+        pass_copy(chips[i]).start()
+        if i > 0:
+            text_merge(chips[i - 1])
+            tshare_copy(chips[i - 1]).start()
     text_merge(x)
-    wd_pass((0, 1))
+    wd_pass(0)
 
     def image_part(p):
-        part = dot_nn(tlow_t[...], grads[:, p * 256 : (p + 1) * 256])
+        part = sum(
+            dot_nn(tlow_t[:, rows(chips[i] * 256, 256)], parts[i][:, p * 256 : (p + 1) * 256]) for i in range(4)
+        )
         for j in (0, 1):
             dz, dy = ORDER[2 * p + j]
             block = part[:, j * 128 : (j + 1) * 128].astype(BF16)
@@ -472,11 +459,10 @@
                 image_far(n + 4, swap).start()
 
 
+    wd_pass(1)
     h_copy.wait_recv()
 
-    for j in range(-1, 5):
-        for which in both:
-            wd(which, j, 1 - core).wait_recv()
+    wd_wait(0)
 
     def home(q):
         return (q // 2 + 4 - x) % 4, q % 2
@@ -485,7 +471,7 @@
         h = jnp.where(r // 4 == section, hin[rows(me * 128), :], hother[...])
         slope_own[r] = slope_of(dot_nn(h, wi_all[home(r)]))
 
-    loop(8, own_block)
+    loop(8, own_block, 4)
 
     def tshare_sum(i, acc):
         chip = (x + i) % 4
@@ -496,28 +482,43 @@
     unit, length = unit_rows(text[rows(me * 128), :])
     gown[0] = unit_backward(unit, length, total).astype(BF16)
 
-    def g_copy(layer, lo, sems):
-        to = {"section": layer, "mp": lo * 2 + core}
-        return copy_to(gown.at[1 - layer], gbuf.at[me], sems.at[lo], g_rs.at[me], to)
+    sibling = x + 1 - 2 * (x % 2)
+
+    def g_copy(layer, half, sems):
+        at = pl.ds(half * 64, 64)
+        to = jnp.where(section == layer, sibling, 3 - x) * 2 + core
+        return copy_to(gown.at[1 - layer, at], gbuf.at[me, at], sems.at[half], g_rs.at[me * 2 + half], line(to))
 
     def g_send(layer, sems):
-        for lo in (0, 1):
-            pl.when(x != layer * 2 + lo)(lambda lo=lo: g_copy(layer, lo, sems).start())
+        for half in both:
+            g_copy(layer, half, sems).start()
 
         @pl.when(section == layer)
         def _():
             gbuf[me] = gown[1 - layer]
 
+    def g_forward(half):
+        q = (3 - x) * 2 + core
+        block = gbuf.at[q, pl.ds(half * 64, 64)]
+        return copy_to(block, block, gf_ss.at[half], g_rs.at[q * 2 + half], line(sibling * 2 + core))
+
+    def g_arrive(chip):
+        q = chip * 2 + core
+        for half in both:
+            block = gbuf.at[q, pl.ds(half * 64, 64)]
+            copy_to(block, block, gf_ss.at[0], g_rs.at[q * 2 + half], line(me)).wait_recv()
+
+    def order_of(i):
+        return jnp.where(i == 0, x, jnp.where(i == 1, sibling, jnp.where(i == 2, 3 - x, 3 - sibling)))
+
     def g_pass(i):
-        q = ((x + i) % 4) * 2 + core
-        return copy_to(gbuf.at[q], gbuf.at[q], gp_ss.at[i], g_rs.at[q], line(x * 2 + 1 - core))
-
-    def g_arrive(q):
-        copy_to(gbuf.at[q], gbuf.at[q], gp_ss.at[0], g_rs.at[q], line(me)).wait_recv()
-
-    def g_relay(i):
-        g_arrive(((x + i) % 4) * 2 + core)
-        g_pass(i).start()
+        chip = order_of(i)
+        block = gbuf.at[chip * 2 + core]
+        return copy_to(block, block, gp_ss.at[i], gp_rs.at[chip], line(x * 2 + 1 - core))
+
+    def g_passed(chip):
+        block = gbuf.at[chip * 2 + 1 - core]
+        copy_to(block, block, gp_ss.at[0], gp_rs.at[chip], line(me)).wait_recv()
 
     def chain(layer):
         g = gown[1 - layer]
@@ -530,9 +531,11 @@
 
         return lax.fori_loop(0, 4, step, g.astype(F32)).astype(BF16)
 
+    wd_wait(1)
     g_send(1, g1_ss)
     gown[1] = chain(1)
     g_send(0, g0_ss)
+    loop(4, own_block)
     image_relay()
     lowest = chain(0)
     gin[0] = lowest[:, :256]
@@ -550,15 +553,50 @@
         for far in (2, 1, 3):
             image_near(swap, far).start()
 
-    g_pass(0).start()
-    loop(4, g_relay, 1)
-    loop(8, lambda i: in_copy(i).start(), 1)
-    inbuf[me] = gin[section]
-    for swap in both:
-        image_fold(swap)
-    loop(4, lambda i: g_arrive(((x + i) % 4) * 2 + 1 - core))
-
-    full = gbuf[...].reshape(1024, 512)
+    def weight_rows_of(i):
+        chip = order_of(i)
+        g_passed(chip)
+        at = rows(chip * 256, 256)
+        g = gbuf[pl.ds(2 * chip, 2)].reshape(256, 512)
+        out_part = dot_tn(g, act[at, :])
+        pre_grad = (dot_nt(g, wo_all[0, core]) * slope[at, :]).astype(BF16)
+        in_part = dot_nn(hin_t[:, at], pre_grad)
+
+        @pl.when(i == 0)
+        def _():
+            wacc[1] = out_part
+            wacc[0] = in_part
+
+        @pl.when(i > 0)
+        def _():
+            wacc[1] += out_part
+            wacc[0] += in_part
+
+    def weight_step(i):
+        @pl.when(i < 4)
+        def _():
+            pl.when(i % 2 == 1)(lambda: g_arrive(order_of(i)))
+            pl.when(i != 2)(lambda: g_pass(i).start())
+
+        @pl.when(i == 4)
+        def _():
+            loop(8, lambda k: in_copy(k).start(), 1)
+            inbuf[me] = gin[section]
+
+        @pl.when(i == 2)
+        def _():
+            for swap in both:
+                image_fold(swap)
+
+        pl.when(i > 0)(lambda: weight_rows_of(i - 1))
+
+    for half in both:
+        q = (3 - x) * 2 + core
+        block = gbuf.at[q, pl.ds(half * 64, 64)]
+        copy_to(block, block, gf_ss.at[0], g_rs.at[q * 2 + half], line(me)).wait_recv()
+        g_forward(half).start()
+    g_pass(2).start()
+    loop(5, weight_step)
 
     def put_weight(which, value):
         for zz in range(4):
@@ -567,12 +605,30 @@
                 wg[which, 0, zz, yy] = block[:, :256]
                 wg[which, 1, yy, zz] = block[:, 256:]
 
-    def weight_far(which, swap, far):
-        n = which * 6 + swap * 3 + 3 - far
-        at = ((y if swap else z) + far) % 4
-        return copy_to(
-            wg.at[which, swap, at], wfar_in.at[which, swap, 3 - far], wf_ss.at[n], wf_rs.at[n], step_of(swap, far)
-        )
+    def weight_far(which, swap, n):
+        first = y if swap else z
+        block = wg.at[which, swap]
+        landed = wfar_in.at[which, swap]
+        src, dst, to = (
+            (block.at[(first + 2) % 4, 0:2], wrelay_in.at[which, swap, 0], 1),
+            (block.at[(first + 2) % 4, 2:4], wrelay_in.at[which, swap, 1], 3),
+            (block.at[(first + 1) % 4, 2:4], landed.at[0, 2:4], 1),
+            (block.at[(first + 3) % 4, 0:2], landed.at[1, 0:2], 3),
+            (wjoined.at[which, swap, 0], landed.at[0, 0:2], 1),
+            (wjoined.at[which, swap, 1], landed.at[1, 2:4], 3),
+        )[n]
+        k = which * 12 + swap * 6 + n
+        return copy_to(src, dst, wf_ss.at[k], wf_rs.at[k], step_of(swap, to))
+
+    def weight_relay(which):
+        for n, far, lo in ((0, 1, 0), (1, 3, 2)):
+            for swap in both:
+                weight_far(which, swap, n).wait_recv()
+                block = wg[which, swap, ((y if swap else z) + far) % 4, lo : lo + 2]
+                wjoined[which, swap, n] = (
+                    block.astype(F32) + wrelay_in[which, swap, n].astype(F32)
+                ).astype(BF16)
+                weight_far(which, swap, n + 4).start()
 
     def weight_near(which, swap, far):
         n = which * 6 + swap * 3 + 3 - far
@@ -581,21 +637,22 @@
             wsum.at[which, swap, at], wnear_in.at[which, swap, 3 - far], wn_ss.at[n], wn_rs.at[n], step_of(1 - swap, far)
         )
 
-    def send_all(step, which):
+    def weight_start(which, messages):
+        for n in messages:
+            for swap in both:
+                weight_far(which, swap, n).start()
+
+    def weight_fold(which):
+        for swap in both:
+            for n in range(2, 6):
+                weight_far(which, swap, n).wait_recv()
+            total = wg[which, swap, y if swap else z].astype(F32)
+            for side in both:
+                total = total + wfar_in[which, swap, side].astype(F32)
+            wsum[which, swap] = total.astype(BF16)
         for far in (2, 1, 3):
             for swap in both:
-                step(which, swap, far).start()
-
-    def weight_fold(which):
-        for swap in both:
-            total = wg[which, swap, y if swap else z].astype(F32)
-            for far in (1, 2, 3):
-                landed = wfar_in.at[which, swap, far - 1]
-                n = which * 6 + swap * 3 + far - 1
-                copy_to(landed, landed, wf_ss.at[n], wf_rs.at[n], {"dp": dp}).wait_recv()
-                total = total + landed[...].astype(F32)
-            wsum[which, swap] = total.astype(BF16)
-        send_all(weight_near, which)
+                weight_near(which, swap, far).start()
 
     def weight_end(which, out):
         for swap in both:
@@ -607,18 +664,15 @@
                 total = total + landed[...].astype(F32)
             out[0, :, swap * 256 : (swap + 1) * 256] = total
 
-    put_weight(1, dot_tn(full, act[...]))
-    send_all(weight_far, 1)
-
-    def back_block(r):
-        at = rows(r * 256, 256)
-        back = dot_nt(gbuf[pl.ds(2 * r, 2)].reshape(256, 512), wo_all[0, core])
-        act[at, :] = (back * slope[at, :]).astype(BF16)
-
-    loop(4, back_block)
-    put_weight(0, dot_nn(hin_t[...], act[...]))
-    send_all(weight_far, 0)
-
+    put_weight(1, wacc[1])
+    weight_start(1, (0, 1))
+    put_weight(0, wacc[0])
+    weight_start(0, (0, 1))
+    weight_start(1, (2, 3))
+    weight_start(0, (2, 3))
+
+    weight_relay(1)
+    weight_relay(0)
     for swap in both:
         total = isum[swap, 0].astype(F32)
         for far in (1, 2, 3):
@@ -668,15 +722,18 @@
             image_far(n, swap).wait_send()
     ihalf_copy.wait_send()
     for layer, sems in ((1, g1_ss), (0, g0_ss)):
-        for lo in (0, 1):
-            pl.when(x != layer * 2 + lo)(lambda lo=lo, layer=layer, sems=sems: g_copy(layer, lo, sems).wait_send())
+        for half in both:
+            g_copy(layer, half, sems).wait_send()
+    for half in both:
+        g_forward(half).wait_send()
     loop(4, lambda i: g_pass(i).wait_send())
     loop(8, lambda i: in_copy(i).wait_send(), 1)
     for which in both:
         for swap in both:
             for far in (1, 2, 3):
-                weight_far(which, swap, far).wait_send()
                 weight_near(which, swap, far).wait_send()
+            for n in range(6):
+                weight_far(which, swap, n).wait_send()
 
 
 def settle(*refs):
@@ -695,7 +752,7 @@
         pltpu.VMEM((1024, 512), BF16),
         pltpu.VMEM((512, 1024), BF16),
         pltpu.VMEM((8, 1024, 256), F32),
-        pltpu.VMEM((1024, 2048), BF16),
+        *[pltpu.VMEM((256, 2048), BF16)] * 4,
         pltpu.VMEM((1024, 128), F32),
         pltpu.VMEM((1024, 128), F32),
         pltpu.VMEM((1024, 128), F32),
@@ -728,8 +785,11 @@
         pltpu.VMEM((2, 128, 256), BF16),
         pltpu.VMEM((2, 128, 512), BF16),
         pltpu.VMEM((8, 128, 256), BF16),
+        pltpu.VMEM((2, 512, 512), F32),
         pltpu.VMEM((2, 2, 4, 4, 32, 256), BF16),
-        pltpu.VMEM((2, 2, 3, 4, 32, 256), BF16),
+        pltpu.VMEM((2, 2, 2, 2, 32, 256), BF16),
+        pltpu.VMEM((2, 2, 2, 2, 32, 256), BF16),
+        pltpu.VMEM((2, 2, 2, 4, 32, 256), BF16),
         pltpu.VMEM((2, 2, 4, 32, 256), BF16),
         pltpu.VMEM((2, 2, 3, 32, 256), BF16),
         dma((5,)),
@@ -741,9 +801,9 @@
         dma((4,)), dma((4,)), dma((4,)), dma((4,)),
         dma((12,)), dma((12,)), dma((6,)), dma((6,)),
         dma((2,)),
-        dma((2,)), dma((2,)), dma((4,)), dma((8,)),
+        dma((2,)), dma((2,)), dma((2,)), dma((16,)), dma((4,)), dma((4,)),
         dma((8,)), dma((8,)),
-        dma((12,)), dma((12,)), dma((12,)), dma((12,)),
+        dma((24,)), dma((24,)), dma((12,)), dma((12,)),
     ]
     results = pl.pallas_call(
         kernel,

time: 79.5 us -> 76.3 us (0.960)
  Pallas kernels: 77.3 us -> 74.9 us
    pallas_call x1, Pallas kernels: 75.3 us -> 72.8 us  [body(): pl.pallas_call(kernel, out_shape=(jax.ShapeDtypeStruct((256, 512), BF16),...]
where the time goes in v4:
time: 76.3 us; the launch traced here: 76.2 us
  Pallas kernels  74.9 us (98%)
  between operations  1.29 us (2%)
    pallas_call x1, Pallas kernels, body(): pl.pallas_call(kernel, out_shape=(jax.ShapeDtypeStruct((256, 512), BF16),...  72.8 us
    pallas_call x1, Pallas kernels, body(): pl.pallas_call(settle, out_shape=tuple((jax.ShapeDtypeStruct(r.shape, r.d...  2.06 us

profile of v4, /device:TPU:1, one launch (start us, length us, event | category | flops | bytes accessed | tf_op | source)
XLA Modules:
  0.0 76.2 jit_solution(2202329387424631698)
XLA Ops:
  1.3 72.8 %shard_map.93 = (bf16[256,512]{1,0:T(8,128)(2,1)}, bf16[1024,256]{1,0:T(8,128)(2,1)}, f32[1,32,512]{2,1,0:T(8,128)}, f32[1,32,512]{2,1,0:T(8,128)}) custom-call(f32[1]{0:T(128)S(6)} %copy.10.scale, bf16[1024,512]{1,0:T(8,128)(2,1)} %text_hbm.1, bf16[256,512]{1,0:T(8,128)(2,1)} %image_hbm.1, bf16[1,1024,512]{2,1,0:T(8,128)(2,1)} %hin_hbm.1, ...), custom_call_target="tpu_custom_call" | custom-call | tf_op jit(solution)/shard_map/pallas_call | solution.py:808
  74.1 2.1 %shard_map.94 = (bf16[256,512]{1,0:T(8,128)(2,1)}, bf16[1024,256]{1,0:T(8,128)(2,1)}, f32[1,32,512]{2,1,0:T(8,128)}, f32[1,32,512]{2,1,0:T(8,128)}) custom-call(bf16[256,512]{1,0:T(8,128)(2,1)} %get-tuple-element.8.refs_0_, bf16[1024,256]{1,0:T(8,128)(2,1)} %get-tuple-element.9.refs_1_, f32[1,32,512]{2,1,0:T(8,128)} %get-tuple-element.10.refs_2_, ...), custom_call_target="tpu_custom_call" | custom-call | tf_op jit(solution)/shard_map/pallas_call | solution.py:823

commit v5 on v4

--- a/solution.py
+++ b/solution.py
@@ -187,21 +187,25 @@
             ref.at[src, core, at], ref.at[dst, core, at], wx_ss.at[n], wx_rs.at[which * 4 + dst], line(chip * 2 + core)
         )
 
-    wx_plan = ((0, 0, 3, right), (1, 0, 1, left), (1, 0, 3, right), (0, 0, 1, left), (0, 3, 2, right), (1, 1, 2, left))
+    wx_plan = ((0, 0, 2, right), (1, 0, 1, left), (1, 0, 2, right), (0, 0, 1, left), (0, 2, 3, right), (1, 1, 3, left))
 
     def wx_wait(which, rel):
         block = weights[which].at[rel, core, weight_rows(0)]
         copy_to(block, block, wx_ss.at[0], wx_rs.at[which * 4 + rel], line(me)).wait_recv()
 
-    def wy(which, j):
+    def wy_block(part, j, turn):
+        which, first, count = ((0, 1, 2), (0, 3, 1), (1, 1, 3))[part]
+        return weights[which].at[pl.ds(first, count), core, weight_rows(turn, j * 64, 64)]
+
+    def wy(part, j):
         dz, dy = AROUND[j]
-        block = weights[which].at[pl.ds(1, 3), core, weight_rows(0, j * 64, 64)]
-        n = which * 4 + j
+        block = wy_block(part, j, 0)
+        n = part * 4 + j
         return copy_to(block, block, wy_ss.at[n], wy_rs.at[n], {"dp": plane(4 - dz, 4 - dy)})
 
-    def wy_wait(which, j):
-        block = weights[which].at[pl.ds(1, 3), core, weight_rows(1, j * 64, 64)]
-        n = which * 4 + j
+    def wy_wait(part, j):
+        block = wy_block(part, j, 1)
+        n = part * 4 + j
         copy_to(block, block, wy_ss.at[n], wy_rs.at[n], {"dp": dp}).wait_recv()
 
     def wd(which, j, side):
@@ -275,22 +279,26 @@
             half_wait(swap, 3, second)
             half_send(swap, 3, second, 1, 0)
             half_wait(swap, 1, second)
-    wx_wait(0, 3)
+    wx_wait(0, 2)
     wx(4, *wx_plan[4]).start()
     wx_wait(1, 1)
     wx(5, *wx_plan[5]).start()
     loop(4, score_pair, 2)
     for swap in both:
+        half_wait(swap, 2, 0)
+    loop(5, score_pair, 4)
+    for swap in both:
         half_wait(swap, 1, 2)
         half_send(swap, 1, 2, 3, 0)
         half_wait(swap, 3, 2)
-    for swap in both:
-        half_wait(swap, 2, 0)
     half_wait(1, 2, 1)
-    loop(6, score_pair, 4)
+    loop(6, score_pair, 5)
     half_wait(0, 2, 1)
     for swap in both:
         half_wait(swap, 2, 3)
+    wx_wait(0, 1)
+    for j in range(4):
+        wy(0, j).start()
     loop(7, score_pair, 6)
     for swap in both:
         half_wait(swap, 2, 2)
@@ -385,19 +393,20 @@
 
     def wd_pass(which):
         for j in range(4):
-            wy_wait(which, j)
+            for part in ((0, 1), (2,))[which]:
+                wy_wait(part, j)
             wd(which, j, core).start()
 
     def wd_wait(which):
         for j in range(-1, 5):
             wd(which, j, 1 - core).wait_recv()
 
+    wx_wait(1, 2)
     for which in both:
-        wx_wait(which, 1 if which == 0 else 3)
-        wx_wait(which, 2)
-    for which in both:
+        wx_wait(which, 3)
+    for part in (1, 2):
         for j in range(4):
-            wy(which, j).start()
+            wy(part, j).start()
     for which in both:
         wd(which, 4, core).start()
     make_grads(0)
@@ -465,7 +474,8 @@
     wd_wait(0)
 
     def home(q):
-        return (q // 2 + 4 - x) % 4, q % 2
+        turn = (q // 2 + 4 - x) % 4
+        return jnp.where(turn == 2, 3, jnp.where(turn == 3, 2, turn)), q % 2
 
     def own_block(r):
         h = jnp.where(r // 4 == section, hin[rows(me * 128), :], hother[...])
@@ -706,10 +716,11 @@
     for n in range(6):
         wx(n, *wx_plan[n]).wait_send()
     for which in both:
-        for j in range(4):
-            wy(which, j).wait_send()
         for j in range(-1, 5):
             wd(which, j, core).wait_send()
+    for part in range(3):
+        for j in range(4):
+            wy(part, j).wait_send()
     for k in range(1, 16):
         cst_copy(k).wait_send()
     loop(8, lambda i: rst_copy(i).wait_send(), 1)
@@ -737,8 +748,12 @@
 
 
 def settle(*refs):
-    for src, dst in zip(refs[:4], refs[4:]):
-        dst[...] = src[...]
+    sems = refs[8]
+    copies = [pltpu.make_async_copy(src, dst, sems.at[n]) for n, (src, dst) in enumerate(zip(refs[:4], refs[4:8]))]
+    for copy in copies:
+        copy.start()
+    for copy in copies:
+        copy.wait()
 
 
 def body(text_feats, image_feats, logit_scale, layer_inputs, w_in, w_out):
@@ -794,7 +809,7 @@
         pltpu.VMEM((2, 2, 3, 32, 256), BF16),
         dma((5,)),
         dma((32,)), dma((64,)),
-        dma((6,)), dma((8,)), dma((8,)), dma((8,)), dma((12,)), dma((12,)),
+        dma((6,)), dma((8,)), dma((12,)), dma((12,)), dma((12,)), dma((12,)),
         dma((2,)),
         dma((8,)), dma((8,)),
         dma((16,)), dma((16,)),
@@ -808,23 +823,25 @@
     results = pl.pallas_call(
         kernel,
         out_shape=(
-            jax.ShapeDtypeStruct((256, 512), BF16),
-            jax.ShapeDtypeStruct((1024, 256), BF16),
-            jax.ShapeDtypeStruct((1, 32, 512), F32),
-            jax.ShapeDtypeStruct((1, 32, 512), F32),
+            pltpu.VMEM((256, 512), BF16),
+            pltpu.VMEM((1024, 256), BF16),
+            pltpu.VMEM((1, 32, 512), F32),
+            pltpu.VMEM((1, 32, 512), F32),
         ),
         in_specs=[pl.BlockSpec(memory_space=pltpu.SMEM)] + [pl.BlockSpec(memory_space=pl.ANY)] * 5,
         out_specs=(vmem,) * 4,
         scratch_shapes=scratch,
         compiler_params=pltpu.CompilerParams(
-            collective_id=0, has_side_effects=True, vmem_limit_bytes=56 * 1024 * 1024
+            collective_id=0, has_side_effects=True, vmem_limit_bytes=54 * 1024 * 1024
         ),
     )(logit_scale, text_feats, image_feats, layer_inputs, w_in, w_out)
+    results = [pltpu.with_memory_space_constraint(r, pltpu.VMEM) for r in results]
     return pl.pallas_call(
         settle,
         out_shape=tuple(jax.ShapeDtypeStruct(r.shape, r.dtype) for r in results),
         in_specs=[vmem] * 4,
-        out_specs=(vmem,) * 4,
+        out_specs=(pl.BlockSpec(memory_space=pl.ANY),) * 4,
+        scratch_shapes=[dma((4,))],
     )(*results)
 
 

time: 76.3 us -> 74 us (0.970); the launches traced: 76.2 us -> 73 us
  Pallas kernels: 74.9 us -> 71.5 us
    pallas_call x1, Pallas kernels: 72.8 us -> 70.6 us  [body(): pl.pallas_call(kernel, out_shape=(pltpu.VMEM((256, 512), BF16), pltpu.VME...]
    pallas_call x1, Pallas kernels: 2.06 us -> 0.95 us  [body(): pl.pallas_call(settle, out_shape=tuple((jax.ShapeDtypeStruct(r.shape, r.d...]
where the time goes in v5:
time: 74 us; the launch traced here: 73 us
  Pallas kernels  71.5 us (97%)
  between operations  1.45 us (2%)
    pallas_call x1, Pallas kernels, body(): pl.pallas_call(kernel, out_shape=(pltpu.VMEM((256, 512), BF16), pltpu.VME...  70.6 us

profile of v5, /device:TPU:1, one launch (start us, length us, event | category | flops | bytes accessed | tf_op | source)
XLA Modules:
  0.0 73.0 jit_solution(13986139578367901104)
XLA Ops:
  1.3 70.6 %shard_map.93 = (bf16[256,512]{1,0:T(8,128)(2,1)S(1)}, bf16[1024,256]{1,0:T(8,128)(2,1)S(1)}, f32[1,32,512]{2,1,0:T(8,128)S(1)}, f32[1,32,512]{2,1,0:T(8,128)S(1)}) custom-call(f32[1]{0:T(128)S(6)} %copy.10.scale, bf16[1024,512]{1,0:T(8,128)(2,1)} %text_hbm.1, bf16[256,512]{1,0:T(8,128)(2,1)} %image_hbm.1, bf16[1,1024,512]{2,1,0:T(8,128)(2,1)} %hin_hbm.1, ...), custom_call_target="tpu_custom_call" | custom-call | tf_op jit(solution)/shard_map/pallas_call | solution.py:823
  71.9 0.9 %shard_map.94 = (bf16[256,512]{1,0:T(8,128)(2,1)}, bf16[1024,256]{1,0:T(8,128)(2,1)}, f32[1,32,512]{2,1,0:T(8,128)}, f32[1,32,512]{2,1,0:T(8,128)}) custom-call(bf16[256,512]{1,0:T(8,128)(2,1)S(1)} %get-tuple-element.8.refs_0_, bf16[1024,256]{1,0:T(8,128)(2,1)S(1)} %get-tuple-element.9.refs_1_, f32[1,32,512]{2,1,0:T(8,128)S(1)} %get-tuple-element.10.refs_2_, ...), custom_call_target="tpu_custom_call" | custom-call | tf_op jit(solution)/shard_map/pallas_call | solution.py:839

commit v6 on v5

--- a/solution.py
+++ b/solution.py
@@ -170,7 +170,7 @@
         dz, dy = flip(swap, first, second)
         ag_wait(dz, dy, lo + 64 * swap, size)
 
-    for to in ((0, 1), (0, 3), (1, 0), (3, 0)):
+    for to in ((0, 1), (0, 3), (1, 0), (3, 0), (0, 2)):
         for swap in (0, 1):
             half_send(swap, 0, 0, *to)
 
@@ -260,8 +260,6 @@
     for swap in both:
         half_wait(swap, 0, 1)
         half_wait(swap, 0, 3)
-        half_send(swap, 0, 1, 0, 3, 0, 32)
-        half_send(swap, 0, 3, 0, 1, 32, 32)
     for swap in both:
         spread(swap, 0, 1)
         spread(swap, 0, 3)
@@ -271,8 +269,7 @@
         half_wait(swap, 3, 0)
     loop(2, score_pair)
     for swap in both:
-        half_wait(swap, 0, 2, 0, 32)
-        half_wait(swap, 0, 2, 32, 32)
+        half_wait(swap, 0, 2)
         spread(swap, 0, 2)
     for swap in both:
         for second in (1, 3):
@@ -681,35 +678,6 @@
     weight_start(1, (2, 3))
     weight_start(0, (2, 3))
 
-    weight_relay(1)
-    weight_relay(0)
-    for swap in both:
-        total = isum[swap, 0].astype(F32)
-        for far in (1, 2, 3):
-            landed = inear_in.at[swap, far - 1]
-            copy_to(landed, landed, ir_ss.at[0], ir_rs.at[swap * 3 + far - 1], {"dp": dp}).wait_recv()
-            total = total + landed[...].astype(F32)
-        ifull[:, swap * 256 : (swap + 1) * 256] = total.T
-    total = ifull[...] * mult
-    image_unit, image_len = unit_rows(image[...])
-    ihalf[0] = unit_backward(image_unit, image_len, total).astype(BF16)
-    ihalf_copy = copy_to(ihalf.at[0], ihalf.at[1], ih_s.at[0], ih_s.at[1], line(twin))
-    ihalf_copy.start()
-    weight_fold(1)
-
-    def in_wait(i):
-        q = (me + i) % 8
-        copy_to(gin.at[0], inbuf.at[q], in_ss.at[i], in_rs.at[q], line(me)).wait_recv()
-
-    loop(8, in_wait, 1)
-    input_out[...] = inbuf[...].reshape(1024, 256)
-
-    weight_fold(0)
-    image_out[rows(section * 128), :] = ihalf[0]
-    ihalf_copy.wait_recv()
-    image_out[rows((1 - section) * 128), :] = ihalf[1]
-    weight_end(1, second_out)
-    weight_end(0, first_out)
     for copy in sends:
         copy.wait_send()
     h_copy.wait_send()
@@ -726,6 +694,35 @@
     loop(8, lambda i: rst_copy(i).wait_send(), 1)
     loop(4, lambda i: pass_copy(i).wait_send())
     loop(4, lambda i: tshare_copy((x + i) % 4).wait_send(), 1)
+    weight_relay(1)
+    weight_relay(0)
+    for swap in both:
+        total = isum[swap, 0].astype(F32)
+        for far in (1, 2, 3):
+            landed = inear_in.at[swap, far - 1]
+            copy_to(landed, landed, ir_ss.at[0], ir_rs.at[swap * 3 + far - 1], {"dp": dp}).wait_recv()
+            total = total + landed[...].astype(F32)
+        ifull[:, swap * 256 : (swap + 1) * 256] = total.T
+    total = ifull[...] * mult
+    image_unit, image_len = unit_rows(image[...])
+    ihalf[0] = unit_backward(image_unit, image_len, total).astype(BF16)
+    ihalf_copy = copy_to(ihalf.at[0], ihalf.at[1], ih_s.at[0], ih_s.at[1], line(twin))
+    ihalf_copy.start()
+    weight_fold(1)
+
+    def in_wait(i):
+        q = (me + i) % 8
+        copy_to(gin.at[0], inbuf.at[q], in_ss.at[i], in_rs.at[q], line(me)).wait_recv()
+
+    loop(8, in_wait, 1)
+    input_out[...] = inbuf[...].reshape(1024, 256)
+
+    weight_fold(0)
+    image_out[rows(section * 128), :] = ihalf[0]
+    ihalf_copy.wait_recv()
+    image_out[rows((1 - section) * 128), :] = ihalf[1]
+    weight_end(1, second_out)
+    weight_end(0, first_out)
     for swap in both:
         for far in (1, 2, 3):
             image_near(swap, far).wait_send()

time: 74 us -> 73.7 us (level)
  no operation moved by 1% of the time
where the time goes in v6:
time: 73.7 us; the launch traced here: 72.6 us
  Pallas kernels  71.2 us (97%)
  between operations  1.45 us (2%)
    pallas_call x1, Pallas kernels, body(): pl.pallas_call(kernel, out_shape=(pltpu.VMEM((256, 512), BF16), pltpu.VME...  70.2 us

profile of v6, /device:TPU:1, one launch (start us, length us, event | category | flops | bytes accessed | tf_op | source)
XLA Modules:
  0.0 72.6 jit_solution(6567691517272810915)
XLA Ops:
  1.3 70.2 %shard_map.93 = (bf16[256,512]{1,0:T(8,128)(2,1)S(1)}, bf16[1024,256]{1,0:T(8,128)(2,1)S(1)}, f32[1,32,512]{2,1,0:T(8,128)S(1)}, f32[1,32,512]{2,1,0:T(8,128)S(1)}) custom-call(f32[1]{0:T(128)S(6)} %copy.10.scale, bf16[1024,512]{1,0:T(8,128)(2,1)} %text_hbm.1, bf16[256,512]{1,0:T(8,128)(2,1)} %image_hbm.1, bf16[1,1024,512]{2,1,0:T(8,128)(2,1)} %hin_hbm.1, ...), custom_call_target="tpu_custom_call" | custom-call | tf_op jit(solution)/shard_map/pallas_call | solution.py:820
  71.5 0.9 %shard_map.94 = (bf16[256,512]{1,0:T(8,128)(2,1)}, bf16[1024,256]{1,0:T(8,128)(2,1)}, f32[1,32,512]{2,1,0:T(8,128)}, f32[1,32,512]{2,1,0:T(8,128)}) custom-call(bf16[256,512]{1,0:T(8,128)(2,1)S(1)} %get-tuple-element.8.refs_0_, bf16[1024,256]{1,0:T(8,128)(2,1)S(1)} %get-tuple-element.9.refs_1_, f32[1,32,512]{2,1,0:T(8,128)S(1)} %get-tuple-element.10.refs_2_, ...), custom_call_target="tpu_custom_call" | custom-call | tf_op jit(solution)/shard_map/pallas_call | solution.py:836
